TPU v7x, 256 devices: a 4x2x16 block of a 4x16x16 slice. The times are simulated.
256 devices in a mesh: groups: 2 (over y), shard: 16 (over z), head: 4 (over x), pair: 2 (over core).
Axes of the slice: x: 4, y: 2, z: 16, core: 2. Of those that a mesh axis runs over, the one named last changes fastest.
The devices are a block of a 4x16x16 slice.
Arguments:
- prompt_tokens: bfloat16 [2048, 8, 8192], P('shard', 'groups'), parts along dimension 1, may hold values from -48 to 48
- draft_tokens: bfloat16 [2, 8, 8192], P(None, 'groups', 'shard'), parts along dimension 1, may hold values from -48 to 48
- w_query: bfloat16 [8192, 4096], P('shard', ('head', 'pair')), may hold values from -0.0625 to 0.0625
- w_key: bfloat16 [8192, 1024], P('shard', ('head', 'pair')), may hold values from -0.0625 to 0.0625
- w_value: bfloat16 [8192, 1024], P('shard', ('head', 'pair')), may hold values from -0.0625 to 0.0625
- w_out: bfloat16 [4096, 8192], P(('head', 'pair'), 'shard'), may hold values from -0.09375 to 0.09375
- block_map: int32 [64], P('groups'), parts along dimension 0, may hold values from 0 to 31, each once
- prompt_len: int32 [8], P('groups'), parts along dimension 0, may hold values from 512 to 2048
- owner: int32 [8, 32], P(('head', 'pair'), 'groups'), parts along dimension 1, may hold values from 0 to 15, each once within a row
Outputs:
- prefill_out: bfloat16 [2048, 8, 4096], P('shard', 'groups', ('head', 'pair')), parts along dimension 1
- draft_attn: bfloat16 [2, 32, 8, 128], P(None, ('groups', 'shard'), ('head', 'pair')), parts along dimension 1
- decode_out: bfloat16 [2, 8, 8192], P(None, 'groups', ('shard', 'head', 'pair')), parts along dimension 1
There are 2 independent parts, one for each index of `groups`. A program takes and returns all parts, laid end to end along the dimension named above; an argument that names none is the same for every part. Nothing has to cross between parts.
Inputs may be any that keep to these rules, and one draw needn't show every extreme that they name: `owner`: each row is a permutation of the 16 decode slots. `block_map`: a permutation of the 32 blocks.
All inputs are finite; a program needn't handle non-finite values.
Results may differ from a plain program's by a relative error of at most 0.025.
Values may be sent and summed in bfloat16 or wider, within the bound.
A program may use at most 128 MiB of HBM per device.

v0:
```python
import math

import jax
import jax.numpy as jnp
from jax import lax
from jax.sharding import PartitionSpec as P

HEAD_DIM = 128
G = 4
BLK = 64


NEG = -1e30
THETA = 500000.0


def from_everyone(shard, axis):
    devices = lax.axis_size(axis)
    return lax.all_to_all(
        jnp.broadcast_to(shard[None], (devices, *shard.shape)), axis, 0, 0, tiled=True
    )


def laid_out(parts, dim):
    lengths = list(parts.shape[1:])
    lengths[dim] *= parts.shape[0]
    return jnp.moveaxis(parts, 0, dim).reshape(lengths)


def gather_directly(shard, axis, dim):
    parts = from_everyone(shard, axis)
    return laid_out(parts, dim)


def in_one_piece(arrays, axis, dim, along):
    widths = [a.shape[along] for a in arrays]
    both = jnp.concatenate(arrays, axis=along)
    out = lax.all_gather(both, axis, axis=dim, tiled=True)
    return tuple(jnp.split(out, [sum(widths[:k]) for k in range(1, len(widths))], axis=along))


def split_up(shard, dim, devices):
    lengths = shard.shape
    parts = shard.reshape(*lengths[:dim], devices, lengths[dim] // devices, *lengths[dim + 1 :])
    return jnp.moveaxis(parts, dim, 0)


def sent_and_summed(shard, axis, dim):
    devices = lax.axis_size(axis)
    parts = lax.all_to_all(split_up(shard, dim, devices), axis, 0, 0, tiled=True)
    return jnp.sum(parts, axis=0)


def rotate(vec, pos):
    half = vec.shape[-1] // 2
    freq = jnp.exp(jnp.arange(half, dtype=jnp.float32) * (-math.log(THETA) / half))
    angle = pos.astype(jnp.float32)[..., None] * freq
    cosine = jnp.cos(angle)
    sine = jnp.sin(angle)
    first = vec[..., :half]
    second = vec[..., half:]
    return jnp.concatenate([first * cosine - second * sine, second * cosine + first * sine], -1)


def inverse_map(owner):
    slots = owner.shape[1]
    slot_ids = jnp.arange(slots, dtype=jnp.int32)
    match = owner[:, :, None] == slot_ids[None, None, :]
    return jnp.sum(jnp.where(match, slot_ids[None, :, None], 0), axis=1)


def body(prompt_tokens, draft_tokens, w_query, w_key, w_value, w_out, block_map, prompt_len, owner):
    shards = lax.axis_size("shard")
    here = lax.axis_index("shard")
    local_rows, seqs, width = prompt_tokens.shape
    kv_local = w_key.shape[1] // HEAD_DIM
    q_cols = w_query.shape[1]
    k_cols = w_key.shape[1]
    steps = draft_tokens.shape[0]
    slot_count = owner.shape[1]
    per_dev = slot_count // shards
    scale = 1.0 / math.sqrt(HEAD_DIM)
    slot_pos = jnp.repeat(block_map, BLK) * BLK + jnp.tile(
        jnp.arange(BLK, dtype=jnp.int32), 2 * shards
    )
    query_pos = lax.dynamic_slice_in_dim(slot_pos, here * local_rows, local_rows)
    drafts = gather_directly(draft_tokens, "shard", 2)
    all_rows = jnp.concatenate(
        [prompt_tokens.reshape(local_rows * seqs, width), drafts.reshape(steps * seqs, width)], 0
    )
    pieces = in_one_piece((w_query, w_key, w_value), "shard", 0, 1)
    folded = tuple(
        (jnp.dot(all_rows, piece, preferred_element_type=jnp.float32) for piece in pieces)
    )
    whole = jnp.concatenate(folded, 1)
    prompt_proj = whole[: local_rows * seqs]
    draft_proj = whole[local_rows * seqs :]

    def split(proj, lead):
        query = proj[:, :q_cols].reshape(lead + (kv_local, G, HEAD_DIM))
        key = proj[:, q_cols : q_cols + k_cols].reshape(lead + (kv_local, HEAD_DIM))
        value = proj[:, q_cols + k_cols :].reshape(lead + (kv_local, HEAD_DIM))
        return (query, key, value)

    prompt_q, prompt_k, prompt_v = split(prompt_proj, (local_rows, seqs))
    prompt_q = rotate(prompt_q, query_pos[:, None, None, None]).astype(jnp.bfloat16)
    prompt_k = rotate(prompt_k, query_pos[:, None, None]).astype(jnp.bfloat16)
    prompt_v = prompt_v.astype(jnp.bfloat16)
    draft_q, draft_k, draft_v = split(draft_proj, (steps, seqs))
    draft_pos = prompt_len[None, :] + jnp.arange(steps, dtype=jnp.int32)[:, None]
    draft_q = rotate(draft_q, draft_pos[:, :, None, None]).astype(jnp.bfloat16)
    draft_k = rotate(draft_k, draft_pos[:, :, None]).astype(jnp.bfloat16)
    draft_v = draft_v.astype(jnp.bfloat16)
    inverse = inverse_map(owner)
    owned = lax.dynamic_slice_in_dim(inverse, here * per_dev, per_dev, 1)
    owned_seq = owned // G

    def pick(piece):
        moved = piece.transpose(2, 1, 0, 3)
        return jnp.take_along_axis(moved, owned_seq[:, :, None, None], axis=1)

    stat_shape = (local_rows, seqs, kv_local, G)
    start_state = (
        jnp.full(stat_shape, NEG, jnp.float32),
        jnp.zeros(stat_shape, jnp.float32),
        jnp.zeros(stat_shape + (HEAD_DIM,), jnp.float32),
    )
    prompt_slots = local_rows * shards
    empty = jnp.zeros((kv_local, per_dev, prompt_slots, HEAD_DIM), jnp.bfloat16)
    start_state = start_state + (empty, empty)
    key_piece, value_piece = in_one_piece((prompt_k, prompt_v), "shard", 0, 1)
    scores = (
        jnp.einsum("rshgd,nshd->rshgn", prompt_q, key_piece, preferred_element_type=jnp.float32)
        * scale
    )
    valid = (slot_pos[None, None, :] <= query_pos[:, None, None]) & (
        slot_pos[None, None, :] < prompt_len[None, :, None]
    )
    valid = valid[:, :, None, None, :]
    top = start_state[0]
    new_top = jnp.maximum(top, jnp.max(jnp.where(valid, scores, NEG), -1))
    weight = jnp.where(valid, jnp.exp(scores - new_top[..., None]), 0.0)
    total = jnp.sum(weight, -1)
    mixed = jnp.einsum(
        "rshgn,nshd->rshgd",
        weight.astype(jnp.bfloat16),
        value_piece,
        preferred_element_type=jnp.float32,
    )
    kept_k = pick(key_piece)
    kept_v = pick(value_piece)
    prefill_out = (mixed / total[..., None]).astype(jnp.bfloat16).reshape(local_rows, seqs, q_cols)
    cache_k, cache_v = (kept_k, kept_v)
    pair_q = draft_q.transpose(2, 1, 3, 0, 4).reshape(kv_local, seqs * G, steps, HEAD_DIM)
    own_q = jnp.take_along_axis(pair_q, owned[:, :, None, None], axis=1)
    own_k = jnp.take_along_axis(draft_k.transpose(2, 1, 0, 3), owned_seq[:, :, None, None], axis=1)
    own_v = jnp.take_along_axis(draft_v.transpose(2, 1, 0, 3), owned_seq[:, :, None, None], axis=1)
    own_len = jnp.take(prompt_len, owned_seq)
    old = jnp.einsum("hjtd,hjpd->hjtp", own_q, cache_k, preferred_element_type=jnp.float32) * scale
    old_valid = (slot_pos[None, None, :] < own_len[:, :, None])[:, :, None, :]
    new = jnp.einsum("hjtd,hjud->hjtu", own_q, own_k, preferred_element_type=jnp.float32) * scale
    steps_row = jnp.arange(steps, dtype=jnp.int32)
    new_valid = (steps_row[None, :] <= steps_row[:, None])[None, None, :, :]
    top = jnp.maximum(
        jnp.max(jnp.where(old_valid, old, NEG), -1), jnp.max(jnp.where(new_valid, new, NEG), -1)
    )[..., None]
    w_old = jnp.where(old_valid, jnp.exp(old - top), 0.0)
    w_new = jnp.where(new_valid, jnp.exp(new - top), 0.0)
    total = jnp.sum(w_old, -1) + jnp.sum(w_new, -1)
    mixed = jnp.einsum(
        "hjtp,hjpd->hjtd", w_old.astype(jnp.bfloat16), cache_v, preferred_element_type=jnp.float32
    )
    mixed = mixed + jnp.einsum(
        "hjtu,hjud->hjtd", w_new.astype(jnp.bfloat16), own_v, preferred_element_type=jnp.float32
    )
    attn = (mixed / total[..., None]).astype(jnp.bfloat16)
    draft_attn = attn.transpose(2, 1, 0, 3)
    every = gather_directly(draft_attn, "shard", 1)
    by_head = every.transpose(2, 1, 0, 3)
    by_pair = jnp.take_along_axis(by_head, owner[:, :, None, None], axis=1)
    by_pair = by_pair.reshape(kv_local, seqs, G, steps, HEAD_DIM)
    out_rows = w_out.reshape(kv_local, G, HEAD_DIM, w_out.shape[1])
    partial_out = jnp.einsum(
        "hbgtd,hgdc->tbc", by_pair, out_rows, preferred_element_type=jnp.float32
    )
    decode_out = sent_and_summed(partial_out, ("head", "pair"), 2).astype(jnp.bfloat16)
    return (prefill_out, draft_attn, decode_out)


def solution(mesh):
    placed = (
        P("shard", "groups", None),
        P(None, "groups", "shard"),
        P("shard", ("head", "pair")),
        P("shard", ("head", "pair")),
        P("shard", ("head", "pair")),
        P(("head", "pair"), "shard"),
        P("groups"),
        P("groups"),
        P(("head", "pair"), "groups"),
    )
    return jax.shard_map(
        body,
        mesh=mesh,
        in_specs=placed,
        out_specs=(
            P("shard", "groups", ("head", "pair")),
            P(None, ("groups", "shard"), ("head", "pair"), None),
            P(None, "groups", ("shard", "head", "pair")),
        ),
        check_vma=False,
    )
```

profile of v0, /device:TPU:33, one launch (start us, length us, event | category | flops | bytes accessed | tf_op | source)
XLA Modules:
  0.0 311.4 jit_solution(16551148114397866005)
XLA Ops:
  7.3 2.2 pad_maximum_fusion
  9.6 1.4 broadcast_in_dim.148
  11.0 24.6 %all-to-all-start = ((bf16[16,2,4,512]{3,2,1,0:T(4,128)(2,1)}), bf16[16,2,4,512]{3,2,1,0:T(4,128)(2,1)S(1)}, u32[]{:S(2)}, u32[]{:S(2)}) async-start(bf16[16,2,4,512]{3,2,1,0:T(4,128)(2,1)} %broadcast_in_dim.148), calls=%async_computation | async-start | bytes 262144 | tf_op jit(solution)/shard_map/all_to_all | solution.py:19
  35.7 12.5 %reshape.731 = bf16[512,8192]{1,0:T(8,128)(2,1)} reshape(bf16[128,4,8192]{2,1,0:T(4,128)(2,1)} %param.13) | data formatting | bytes 16777216 | tf_op jit(solution)/shard_map/reshape | solution.py:89
  48.2 7.6 %constant_dynamic-update-slice_fusion.1 = bf16[520,8192]{1,0:T(8,128)(2,1)} fusion(bf16[512,8192]{1,0:T(8,128)(2,1)} %reshape.731), kind=kLoop, calls=%fused_computation.87 | loop fusion | bytes 16777216
  56.6 0.7 constant_dynamic-update-slice_fusion
  57.2 115.4 %all-gather.3.cloned.1.call-done = bf16[8192,768]{1,0:T(8,128)(2,1)} async-done(((bf16[512,768]{1,0:T(8,128)(2,1)}), bf16[8192,768]{1,0:T(8,128)(2,1)}) %all-gather.3.cloned.1.call-update) | async-done | bytes 12582928 | tf_op jit(solution)/shard_map/all_gather | solution.py:38
  172.7 6.5 %fusion.13 = f32[520,128]{1,0:T(8,128)S(1)} fusion(bf16[520,8192]{1,0:T(8,128)(2,1)} %constant_dynamic-update-slice_fusion, bf16[8192,768]{1,0:T(8,128)(2,1)} %all-gather.3.cloned.1.call-done), kind=kOutput, calls=%fused_computation.16 | convolution fusion | flops 1090519040 | bytes 10883072 | tf_op jit(solution)/shard_map/dot_general | solution.py:93
  179.5 4.2 %fusion.25 = bf16[520,128]{1,0:T(8,128)(2,1)S(1)} fusion(bf16[520,8192]{1,0:T(8,128)(2,1)S(1)} %copy-done.2, bf16[8192,768]{1,0:T(8,128)(2,1)} %all-gather.3.cloned.1.call-done), kind=kOutput, calls=%fused_computation.27 | convolution fusion | flops 1090585600 | bytes 10749952 | tf_op jit(solution)/shard_map/dot_general | solution.py:93
  183.8 0.8 pad_maximum_fusion.1
  190.1 0.6 dynamic-slice.17
  191.3 0.7 reduce.14
  193.2 1.6 broadcast_and_fusion
  194.9 9.9 %fusion.6 = f32[520,512]{1,0:T(8,128)S(1)} fusion(bf16[520,8192]{1,0:T(8,128)(2,1)} %constant_dynamic-update-slice_fusion, bf16[8192,768]{1,0:T(8,128)(2,1)} %all-gather.3.cloned.1.call-done), kind=kOutput, calls=%fused_computation.9 | convolution fusion | flops 4362076160 | bytes 17973248 | tf_op jit(solution)/shard_map/dot_general | solution.py:93
  204.8 1.0 slice.116
  206.0 1.6 reshape.735
  208.0 0.6 fusion.83
  208.7 0.7 fusion.34
  209.4 41.8 %all-gather.5.cloned.1.call-done = bf16[2048,8,1,128]{3,0,1,2:T(8,128)(2,1)} async-done(((bf16[128,8,1,128]{3,0,1,2:T(8,128)(2,1)}), bf16[2048,8,1,128]{3,0,1,2:T(8,128)(2,1)}) %all-gather.5.cloned.1.call-update) | async-done | bytes 4194320 | tf_op jit(solution)/shard_map/all_gather | solution.py:38
  251.2 2.5 slice_bitcast_fusion
  254.7 0.6 broadcast_in_dim.167
  255.4 6.6 %all-to-all-start.1 = ((bf16[16,2,1,1,128]{4,1,3,2,0:T(2,128)(2,1)}), bf16[16,2,1,1,128]{4,1,3,2,0:T(2,128)(2,1)S(1)}, u32[]{:S(2)}, u32[]{:S(2)}) async-start(bf16[16,2,1,1,128]{4,1,3,2,0:T(2,128)(2,1)} %broadcast_in_dim.167), calls=%async_computation.1 | async-start | bytes 16384 | tf_op jit(solution)/shard_map/all_to_all | solution.py:19
  262.0 4.0 %fusion = (f32[128,4,4]{0,2,1:T(4,128)S(1)}, f32[4,2048,128,4]{2,1,3,0:T(8,128)S(1)}) fusion(pred[128,4,2048]{0,2,1:T(8,128)(4,1)S(1)} %broadcast_and_fusion, bf16[128,4,4,64]{3,0,2,1:T(8,128)(2,1)S(1)} %get-tuple-element.72, bf16[128,4,4,64]{3,0,2,1:T(8,128)(2,1)S(1)} %get-tuple-element.71, bf16[2048,8,1,128]{3,0,1,2:T(8,128)(2,1)} %all-gather.5.cloned.1.call-done), kind=kOutput, calls=%fused_computation.3 | convolution fusion | flops 1087371264 | bytes 20455424 | tf_op jit(solution)/shard_map/rshgd,nshd->rshgn/dot_general | solution.py:133
  266.0 5.7 %copy-done.1 = f32[4,2048,128,4]{2,1,3,0:T(8,128)} copy-done((f32[4,2048,128,4]{2,1,3,0:T(8,128)}, f32[4,2048,128,4]{2,1,3,0:T(8,128)S(1)}, u32[]{:S(2)}) %copy-start.1) | copy-done | bytes 16777240
  271.7 3.6 %fusion.3 = f32[128,4,4]{0,2,1:T(4,128)S(1)} fusion(f32[4,2048,128,4]{2,1,3,0:T(8,128)S(1)} %get-tuple-element.90, f32[128,4,4]{0,2,1:T(4,128)S(1)} %broadcast_maximum_fusion, pred[128,4,2048]{0,2,1:T(8,128)(4,1)S(1)} %broadcast_and_fusion), kind=kLoop, calls=%fused_computation.6 | loop fusion | flops 16775168 | bytes 17842176 | tf_op jit(solution)/shard_map/reduce_sum | solution.py:143
  275.4 0.6 gather_fusion
  276.3 0.7 reshape.915
  277.0 14.8 %all-to-all-start.2 = ((f32[8,1,512]{2,1,0:T(1,128)}), f32[8,1,512]{2,1,0:T(1,128)S(1)}, u32[]{:S(2)}, u32[]{:S(2)}) async-start(f32[8,1,512]{2,1,0:T(1,128)} %reshape.915), calls=%async_computation.2 | async-start | bytes 32768 | tf_op jit(solution)/shard_map/all_to_all | solution.py:50
  291.8 9.7 %divide_convert_fusion = bf16[128,4,1,4,128]{0,4,3,1,2:T(8,128)(2,1)S(1)} fusion(f32[4,2048,128,4]{2,1,3,0:T(8,128)} %copy-done.1, f32[128,4,4]{0,2,1:T(4,128)S(1)} %broadcast_maximum_fusion, pred[128,4,2048]{0,2,1:T(8,128)(4,1)S(1)} %broadcast_and_fusion, bf16[2048,8,1,128]{3,0,1,2:T(8,128)(2,1)} %all-gather.5.cloned.1.call-done, f32[128,4,4]{0,2,1:T(4,128)S(1)} %fusion.3), kind=kOutput, calls=%fused_computation.33 | convolution fusion | flops 1091043328 | bytes 20463616 | tf_op jit(solution)/shard_map/rshgn,nshd->rshgd/dot_general | solution.py:144
  301.5 1.2 copy.106
  303.2 0.7 reduce.15
  304.0 0.6 reduce_sum.49
  (78 shorter events, 5.9 us)
Async XLA Ops:
  7.2 268.9 %copy-start = (bf16[512,512]{1,0:T(8,128)(2,1)S(1)}, bf16[512,512]{1,0:T(8,128)(2,1)}, u32[]{:S(2)}) copy-start(bf16[512,512]{1,0:T(8,128)(2,1)} %param.18) | copy-start | bytes 1572868
  7.2 165.5 %all-gather.3.cloned.1.call-start = ((), (), s32[]{:S(2)}) async-start(), calls=%async_computation.3 | async-start | bytes 13369344 | tf_op jit(solution)/shard_map/all_gather | solution.py:38
  11.0 37.3 %copy-start.6 = (s32[32]{0:T(128)S(1)}, s32[32]{0:T(128)}, u32[]{:S(2)}) copy-start(s32[32]{0:T(128)} %param.19) | copy-start | bytes 388
  11.0 45.5 %all-to-all-start = ((bf16[16,2,4,512]{3,2,1,0:T(4,128)(2,1)}), bf16[16,2,4,512]{3,2,1,0:T(4,128)(2,1)S(1)}, u32[]{:S(2)}, u32[]{:S(2)}) async-start(bf16[16,2,4,512]{3,2,1,0:T(4,128)(2,1)} %broadcast_in_dim.148), calls=%async_computation | async-start | bytes 262144 | tf_op jit(solution)/shard_map/all_to_all | solution.py:19
  35.6 215.6 %all-gather.5.cloned.1.call-start = ((), (), s32[]{:S(2)}) async-start(), calls=%async_computation.4 | async-start | bytes 4456448 | tf_op jit(solution)/shard_map/all_gather | solution.py:38
  172.7 6.8 %copy-start.2 = (bf16[520,8192]{1,0:T(8,128)(2,1)S(1)}, bf16[520,8192]{1,0:T(8,128)(2,1)}, u32[]{:S(2)}) copy-start(bf16[520,8192]{1,0:T(8,128)(2,1)} %constant_dynamic-update-slice_fusion) | copy-start | bytes 25559044
  179.2 15.6 %copy-start.3 = (f32[520,128]{1,0:T(8,128)}, f32[520,128]{1,0:T(8,128)S(1)}, u32[]{:S(2)}) copy-start(f32[520,128]{1,0:T(8,128)S(1)} %fusion.13) | copy-start | bytes 798724
  179.5 5.2 %copy-start.7 = (s32[1,16]{1,0:T(1,128)S(1)}, s32[1,16]{1,0:T(1,128)}, u32[]{:S(2)}) copy-start(s32[1,16]{1,0:T(1,128)} %param.21) | copy-start | bytes 196
  179.5 10.5 %copy-start.4 = (s32[4]{0:T(128)S(1)}, s32[4]{0:T(128)}, u32[]{:S(2)}) copy-start(s32[4]{0:T(128)} %param.20) | copy-start | bytes 52
  194.9 12.7 %slice-start = ((f32[520,128]{1,0:T(8,128)}), f32[8,128]{1,0:T(8,128)S(1)}, s32[]{:S(2)}) async-start(f32[520,128]{1,0:T(8,128)} %copy-done.3), calls=%async_computation.5 | async-start | bytes 8192 | tf_op jit(solution)/shard_map/slice | solution.py:101
  254.7 11.3 %copy-start.5 = (bf16[2,128]{1,0:T(2,128)(2,1)}, bf16[2,128]{1,0:T(2,128)(2,1)S(1)}, u32[]{:S(2)}) copy-start(bf16[2,128]{1,0:T(2,128)(2,1)S(1)} %fusion.29) | copy-start | bytes 1540
  255.4 19.9 %all-to-all-start.1 = ((bf16[16,2,1,1,128]{4,1,3,2,0:T(2,128)(2,1)}), bf16[16,2,1,1,128]{4,1,3,2,0:T(2,128)(2,1)S(1)}, u32[]{:S(2)}, u32[]{:S(2)}) async-start(bf16[16,2,1,1,128]{4,1,3,2,0:T(2,128)(2,1)} %broadcast_in_dim.167), calls=%async_computation.1 | async-start | bytes 16384 | tf_op jit(solution)/shard_map/all_to_all | solution.py:19
  266.0 5.7 %copy-start.1 = (f32[4,2048,128,4]{2,1,3,0:T(8,128)}, f32[4,2048,128,4]{2,1,3,0:T(8,128)S(1)}, u32[]{:S(2)}) copy-start(f32[4,2048,128,4]{2,1,3,0:T(8,128)S(1)} %get-tuple-element.90) | copy-start | bytes 50331652
  277.0 25.6 %all-to-all-start.2 = ((f32[8,1,512]{2,1,0:T(1,128)}), f32[8,1,512]{2,1,0:T(1,128)S(1)}, u32[]{:S(2)}, u32[]{:S(2)}) async-start(f32[8,1,512]{2,1,0:T(1,128)} %reshape.915), calls=%async_computation.2 | async-start | bytes 32768 | tf_op jit(solution)/shard_map/all_to_all | solution.py:50
Sparse Core Ops, SparseCore 0:
  9.8 162.7 all-gather.2
  184.8 66.3 all-gather.4
where the time goes:
time: 312 us; the launch traced here: 311 us
  waiting for transfers between devices  157 us (50%)
  starting transfers between devices  46.2 us (15%)
  local copies, waits for them, and re-layouts  40 us (13%)
  matrix products  35.3 us (11%)
  between operations  19.7 us (6%)
  other arithmetic  12.9 us (4%)
    all_gather x2, waiting for transfers between devices, in_one_piece(): out = lax.all_gather(both, axis, axis=dim, tiled=True)  157 us
    all_to_all x2, starting transfers between devices, from_everyone(): lax.all_to_all(jnp.broadcast_to(shard[None], (devices, *shard.shape)), ax...  31.3 us
    dot_general x3, matrix products, body(): jnp.dot(all_rows, piece, preferred_element_type=jnp.float32)  20.6 us
    unnamed x22, local copies, waits for them, and re-layouts  16 us
    all_to_all x1, starting transfers between devices, sent_and_summed(): lax.all_to_all(split_up(shard, dim, devices), axis, 0, 0, tiled=True)  14.8 us
    reshape x1, local copies, waits for them, and re-layouts, body(): prompt_tokens.reshape(local_rows * seqs, width)  12.5 us
    dot_general x1, matrix products, body(): jnp.einsum('rshgn,nshd->rshgd', weight.astype(jnp.bfloat16), value_piece,...  9.66 us
  transfers between devices with their start and end apart: 5, of which 2 were waited for; matrix products, arithmetic and copies ran while one was open for 19% of the time, Pallas kernels for 0%

commit v1 on v0

v1 whole, which is shorter than its diff:
```python
import functools
import math

import jax
import jax.numpy as jnp
from jax import lax
from jax.experimental import pallas as pl
from jax.experimental.pallas import tpu as pltpu
from jax.sharding import PartitionSpec as P

HEAD_DIM = 128
G = 4
BLK = 64
NEG = -1e30
THETA = 500000.0
MESH = pl.DeviceIdType.MESH
F32 = jnp.float32
BF16 = jnp.bfloat16
FAR = 1 << 30


def rope_tables(pos):
    lane = lax.broadcasted_iota(jnp.int32, (pos.shape[0], HEAD_DIM), 1)
    half = HEAD_DIM // 2
    pair = jnp.where(lane < half, lane, lane - half).astype(F32)
    freq = jnp.exp(pair * (-math.log(THETA) / half))
    angle = pos.astype(F32) * freq
    sine = jnp.sin(angle)
    return jnp.cos(angle), jnp.where(lane < half, -sine, sine)


def rope(v, cosine, sine):
    return v * cosine + pltpu.roll(v, HEAD_DIM // 2, 1) * sine


def kernel(
    shards, heads, pairs,
    x_hbm, d_ref, wq_hbm, wk_hbm, wv_hbm, wo_hbm, map_ref, len_ref, owner_ref,
    out_hbm, dattn_ref, dec_ref,
    buf, xin, xs, dbuf, acc, qbuf, sbuf, pbuf, lbuf, obuf, ostage, oready, cosb, sinb, dcos, dsin, kpos,
    dkv, aflat, lhs, wo, part, parts,
    load_sem, x_sem, out_sem, send_sem, recv_sem, dsend_sem, drecv_sem, psend_sem, precv_sem,
):
    me = lax.axis_index("shard")
    head = lax.axis_index("head")
    pair = lax.axis_index("pair")
    right = lax.rem(me + 1, shards)
    left = lax.rem(me + shards - 1, shards)
    far = shards // 2
    rows, seqs, width = x_hbm.shape
    depth = wq_hbm.shape[0]
    steps = d_ref.shape[0]
    tall = rows * seqs
    drafts = steps * seqs
    keys = shards * rows
    per = rows // BLK
    scale = 1.0 / math.sqrt(HEAD_DIM)
    peers = heads * pairs
    place = head * pairs + pair

    barrier = pltpu.get_barrier_semaphore()
    for z in (left, right):
        pl.semaphore_signal(barrier, inc=1, device_id={"shard": z}, device_id_type=MESH)
    for k in range(1, peers):
        other = lax.rem(place + k, peers)
        pl.semaphore_signal(
            barrier, inc=1, device_id={"head": other // pairs, "pair": other % pairs}, device_id_type=MESH
        )

    sources = {0: wk_hbm, 1: wv_hbm, 2: wq_hbm.at[:, 0:128], 3: wq_hbm.at[:, 128:256],
               6: wq_hbm.at[:, 256:384], 7: wq_hbm.at[:, 384:512]}
    loads = {s: pltpu.make_async_copy(src, buf.at[s, me], load_sem.at[s]) for s, src in sources.items()}
    wo_load = pltpu.make_async_copy(wo_hbm, wo, load_sem.at[4])
    for s in loads:
        loads[s].start()

    def x_load(owner):
        return pltpu.make_async_copy(
            x_hbm.at[:, :, pl.ds(pl.multiple_of(owner * depth, depth), depth)], xin.at[owner], x_sem.at[owner]
        )

    x_load(me).start()

    def start_x(s, _):
        x_load(lax.rem(me + shards - s, shards)).start()

        @pl.when(s < far)
        def _():
            x_load(lax.rem(me + s, shards)).start()

        return 0

    lax.fori_loop(1, far + 1, start_x, 0)
    wo_load.start()

    d_all = d_ref[...].astype(F32)
    dbuf[me] = jnp.concatenate([d_all[t] for t in range(steps)], 0).astype(BF16)

    pl.semaphore_wait(barrier, 2 + peers - 1)

    def hop(stream, way, s):
        owner = lax.rem(me + shards - (s - 1), shards) if way == 0 else lax.rem(me + (s - 1), shards)
        half = depth // 2
        if isinstance(s, int) and s == far:
            ref = buf.at[stream, owner, pl.ds(way * half, half)]
        else:
            ref = buf.at[stream, owner]
        return pltpu.make_async_remote_copy(
            src_ref=ref, dst_ref=ref, send_sem=send_sem.at[stream, way, s - 1], recv_sem=recv_sem.at[stream, way, s - 1],
            device_id={"shard": right if way == 0 else left}, device_id_type=MESH,
        )

    def draft_hop(way, s):
        owner = lax.rem(me + shards - (s - 1), shards) if way == 0 else lax.rem(me + (s - 1), shards)
        return pltpu.make_async_remote_copy(
            src_ref=dbuf.at[owner], dst_ref=dbuf.at[owner], send_sem=dsend_sem.at[way, s - 1],
            recv_sem=drecv_sem.at[way, s - 1], device_id={"shard": right if way == 0 else left}, device_id_type=MESH,
        )

    def launch(phase, s):
        for k in range(2):
            for way in range(2):
                hop(2 * phase + k, way, s).start()

    def arrive(phase, s):
        for k in range(2):
            for way in range(2):
                hop(2 * phase + k, way, s).wait_recv()

    slot_of = {0: 0, 1: 1, 3: 2}

    def multiply(phase, owner, first=False):
        w = jnp.concatenate([buf[2 * phase, owner], buf[2 * phase + 1, owner]], 1)
        got = jnp.dot(xs[owner], w, preferred_element_type=F32)
        for k in range(2):
            slot = 2 * slot_of[phase] + k
            if first:
                acc[slot] = got[:, k * HEAD_DIM : (k + 1) * HEAD_DIM]
            else:
                acc[slot] += got[:, k * HEAD_DIM : (k + 1) * HEAD_DIM]

    def fetch_rows(owner):
        x_load(owner).wait()
        xs[owner, 0:tall] = xin[owner].reshape(tall, depth)
        xs[owner, tall : tall + drafts] = dbuf[owner]

    def ring(phase, local, work, ready_next):
        def step(s, _):
            arrive(phase, s)
            if phase == 0:
                draft_hop(0, s).wait_recv()
                draft_hop(1, s).wait_recv()
            if_last = s == far - 1

            @pl.when(jnp.logical_not(if_last))
            def _():
                launch(phase, s + 1)

            @pl.when(if_last)
            def _():
                launch(phase, far)

            if phase == 0:
                draft_hop(0, s + 1).start()

                @pl.when(jnp.logical_not(if_last))
                def _():
                    draft_hop(1, s + 1).start()

            work(s)
            return 0

        local()
        lax.fori_loop(1, far, step, 0)
        ready_next()
        arrive(phase, far)
        if phase == 0:
            draft_hop(0, far).wait_recv()

    def both(phase):
        def work(s):
            def one(way, _):
                owner = lax.rem(me + shards + (2 * way - 1) * s, shards)
                if phase == 0:
                    fetch_rows(owner)
                multiply(phase, owner)
                return 0

            lax.fori_loop(0, 2, one, 0)

        return work

    opposite = lax.rem(me + far, shards)

    loads[0].wait()
    loads[1].wait()
    launch(0, 1)
    draft_hop(0, 1).start()
    draft_hop(1, 1).start()

    def local0():
        row = lax.broadcasted_iota(jnp.int32, (rows, 1), 0)
        pos = row + map_ref[me * per] * BLK
        for j in range(1, per):
            pos = jnp.where(row >= j * BLK, row - j * BLK + map_ref[me * per + j] * BLK, pos)
        cosb[...], sinb[...] = rope_tables(pos)
        drow = lax.broadcasted_iota(jnp.int32, (drafts, 1), 0)
        dpos = jnp.zeros((drafts, 1), jnp.int32)
        for t in range(steps):
            for b in range(seqs):
                dpos = jnp.where(drow == t * seqs + b, len_ref[b] + t, dpos)
        dcos[...], dsin[...] = rope_tables(dpos)
        for z in range(shards):
            lane = lax.broadcasted_iota(jnp.int32, (seqs, rows), 1)
            where = lane + map_ref[z * per] * BLK
            for j in range(1, per):
                where = jnp.where(lane >= j * BLK, lane - j * BLK + map_ref[z * per + j] * BLK, where)
            lengths = jnp.zeros((seqs, rows), jnp.int32)
            seq = lax.broadcasted_iota(jnp.int32, (seqs, rows), 0)
            for b in range(seqs):
                lengths = jnp.where(seq == b, len_ref[b], lengths)
            kpos[:, z * rows : (z + 1) * rows] = jnp.where(where < lengths, where, FAR)
        fetch_rows(me)
        multiply(0, me, True)

    def next0():
        loads[2].wait()
        loads[3].wait()
        launch(1, 1)

    ring(0, local0, both(0), next0)
    fetch_rows(opposite)
    multiply(0, opposite)

    def own_cache(b, _):
        k = acc[0, pl.ds(b, rows, stride=seqs), :]
        v = acc[1, pl.ds(b, rows, stride=seqs), :]
        at = pl.ds(pl.multiple_of(b * rows, rows), rows)
        buf[4, me, at] = rope(k, cosb[...], sinb[...]).astype(BF16)
        buf[5, me, at] = v.astype(BF16)
        return 0

    lax.fori_loop(0, seqs, own_cache, 0)
    dkv[0] = rope(acc[0, tall : tall + drafts, :], dcos[...], dsin[...]).astype(BF16)
    dkv[1] = acc[1, tall : tall + drafts, :].astype(BF16)

    ring(1, lambda: multiply(1, me, True), both(1), lambda: launch(2, 1))
    multiply(1, opposite)

    def queries(part):
        for b in range(seqs):
            for k in range(2):
                q = acc[2 + 2 * part + k, pl.ds(b, rows, stride=seqs), :]
                qbuf[b, k * rows : (k + 1) * rows] = rope(q, cosb[...], sinb[...]).astype(BF16)
        pieces = []
        dq = [rope(acc[2 + 2 * part + k, tall : tall + drafts, :], dcos[...], dsin[...])
              for k in range(2)]
        for b in range(seqs):
            pieces = [dq[k][t * seqs + b : t * seqs + b + 1] for k in range(2) for t in range(steps)]
            block = jnp.concatenate(pieces + [jnp.zeros((16 - 2 * steps, HEAD_DIM), F32)], 0)
            qbuf[b, 2 * rows : 2 * rows + 16] = block.astype(BF16)

    high = 2 * rows + 16

    def attend(part, b):
        cache_k = buf[4, :, pl.ds(pl.multiple_of(b * rows, rows), rows), :].reshape(keys, HEAD_DIM)
        cache_v = buf[5, :, pl.ds(pl.multiple_of(b * rows, rows), rows), :].reshape(keys, HEAD_DIM)
        q = qbuf[b]
        sbuf[...] = lax.dot_general(q, cache_k, (((1,), (1,)), ((), ())), preferred_element_type=F32)
        q_d = qbuf[b, 2 * rows : high]
        new = lax.dot_general(q_d, dkv[0], (((1,), (1,)), ((), ())), preferred_element_type=F32)
        r = lax.broadcasted_iota(jnp.int32, (16, drafts), 0)
        c = lax.broadcasted_iota(jnp.int32, (16, drafts), 1)
        seen = (lax.rem(c, seqs) == b) & (c // seqs <= lax.rem(r, steps))
        new = jnp.where(seen, new, NEG)
        new_top = jnp.max(new, 1, keepdims=True)
        kp = kpos[pl.ds(b, 1), :]

        def block(at, limit, floor):
            s = sbuf[pl.ds(at, 16), :]
            s = jnp.where(kp <= limit, s, NEG)
            top = jnp.max(s, 1, keepdims=True)
            if floor is not None:
                top = jnp.maximum(top, floor)
            w = jnp.exp((s - top) * scale)
            pbuf[pl.ds(at, 16), :] = w.astype(BF16)
            return top, jnp.sum(w, 1, keepdims=True)

        def prompt_block(i, _):
            at = pl.multiple_of(i * 16, 16)
            row = lax.rem(lax.broadcasted_iota(jnp.int32, (16, 1), 0) + at, rows)
            pos = row + map_ref[me * per] * BLK
            for j in range(1, per):
                pos = jnp.where(row >= j * BLK, row - j * BLK + map_ref[me * per + j] * BLK, pos)
            _, total = block(at, pos, None)
            lbuf[pl.ds(at, 16), :] = jnp.broadcast_to(total, (16, HEAD_DIM))
            return 0

        lax.fori_loop(0, 2 * rows // 16, prompt_block, 0, unroll=4)
        top, total = block(2 * rows, FAR - 1, new_top)
        w_new = jnp.where(seen, jnp.exp((new - top) * scale), 0.0)
        total = total + jnp.sum(w_new, 1, keepdims=True)
        obuf[...] = jnp.dot(pbuf[...], cache_v, preferred_element_type=F32)
        mixed = obuf[2 * rows : high] + jnp.dot(w_new.astype(BF16), dkv[1], preferred_element_type=F32)
        attn = (mixed / total).astype(BF16).astype(F32)
        aflat[pl.ds(pl.multiple_of(b * 2 * G, 2 * G) + part * 2 * steps, 2 * steps), :] = attn[0 : 2 * steps]
        for k in range(2):
            got = obuf[k * rows : (k + 1) * rows] / lbuf[k * rows : (k + 1) * rows]
            ostage[k, pl.ds(b, rows, stride=seqs), :] = got

    def put_out(part):
        for k in range(2):
            oready[:, :, (2 * part + k) * HEAD_DIM : (2 * part + k + 1) * HEAD_DIM] = (
                ostage[k].astype(BF16).reshape(rows, seqs, HEAD_DIM)
            )

    def next2():
        loads[6].wait()
        loads[7].wait()
        launch(3, 1)

    ring(2, lambda: queries(0), lambda s: None, next2)

    def work3(s):
        both(3)(s)

        @pl.when(s <= seqs)
        def _():
            attend(0, s - 1)

    ring(3, lambda: multiply(3, me, True), work3, lambda: put_out(0))
    multiply(3, opposite)
    queries(1)

    def last(b, _):
        attend(1, b)
        return 0

    lax.fori_loop(0, seqs, last, 0)

    wo_load.wait()
    for g in range(G):
        for t in range(steps):
            lhs[t * seqs : (t + 1) * seqs, g * HEAD_DIM : (g + 1) * HEAD_DIM] = aflat[
                pl.ds(g * steps + t, seqs, stride=G * steps), :
            ]
    partial = jnp.dot(lhs[...].astype(BF16), wo[...], preferred_element_type=F32)
    wide = partial.shape[1] // heads
    for h in range(heads):
        part[h] = partial[:, h * wide : (h + 1) * wide]
    parts[place] = part[head]

    def give(k):
        other = lax.rem(place + k, peers)
        return pltpu.make_async_remote_copy(
            src_ref=part.at[other // pairs], dst_ref=parts.at[place], send_sem=psend_sem.at[k], recv_sem=precv_sem.at[k],
            device_id={"head": other // pairs, "pair": other % pairs}, device_id_type=MESH,
        )

    for k in range(1, peers):
        give(k).start()
    put_out(1)
    store = pltpu.make_async_copy(oready, out_hbm, out_sem.at[0])
    store.start()

    r = lax.broadcasted_iota(jnp.int32, (seqs * G * steps, 1), 0)
    mine = jnp.zeros((seqs * G * steps, 1), jnp.int32)
    for p in range(seqs * G):
        mine = jnp.where(r // steps == p, owner_ref[0, p], mine)
    picked = jnp.where(mine == me, aflat[...], 0.0)
    for t in range(steps):
        dattn_ref[t, 0] = jnp.sum(
            jnp.where(lax.rem(r, steps) == t, picked, 0.0), 0, keepdims=True
        ).astype(BF16)

    for k in range(1, peers):
        give(k).wait_recv()
    summed = jnp.sum(parts[...], 0)
    narrow = wide // pairs
    got = summed[:, 0:narrow]
    for j in range(1, pairs):
        got = jnp.where(pair == j, summed[:, j * narrow : (j + 1) * narrow], got)
    for t in range(steps):
        dec_ref[t] = got[t * seqs : (t + 1) * seqs].astype(BF16)

    for k in range(1, peers):
        give(k).wait_send()

    def drain(s, _):
        for stream in range(8):
            for way in range(2):
                hop(stream, way, s).wait_send()
        for way in range(2):
            draft_hop(way, s).wait_send()
        return 0

    lax.fori_loop(1, far, drain, 0)
    for stream in range(8):
        for way in range(2):
            hop(stream, way, far).wait_send()
    draft_hop(0, far).wait_send()
    store.wait()


def body(shards, heads, pairs, x, d, wq, wk, wv, wo, block_map, prompt_len, owner):
    rows, seqs, width = x.shape
    depth = wq.shape[0]
    steps = d.shape[0]
    drafts = steps * seqs
    tall = rows * seqs
    keys = shards * rows
    peers = heads * pairs
    high = 2 * rows + 16
    any_ = pl.BlockSpec(memory_space=pl.ANY)
    vmem = pl.BlockSpec(memory_space=pltpu.VMEM)
    smem = pl.BlockSpec(memory_space=pltpu.SMEM)
    dma = pltpu.SemaphoreType.DMA
    return pl.pallas_call(
        functools.partial(kernel, shards, heads, pairs),
        out_shape=(
            jax.ShapeDtypeStruct((rows, seqs, wq.shape[1]), BF16),
            jax.ShapeDtypeStruct((steps, 1, 1, HEAD_DIM), BF16),
            jax.ShapeDtypeStruct((steps, seqs, wo.shape[1] // peers), BF16),
        ),
        in_specs=[any_, vmem, any_, any_, any_, any_, smem, smem, smem],
        out_specs=(any_, vmem, vmem),
        scratch_shapes=[
            pltpu.VMEM((8, shards, depth, HEAD_DIM), BF16),
            pltpu.VMEM((shards, rows, seqs, depth), BF16),
            pltpu.VMEM((shards, tall + drafts, depth), BF16),
            pltpu.VMEM((shards, drafts, depth), BF16),
            pltpu.VMEM((6, tall + drafts, HEAD_DIM), F32),
            pltpu.VMEM((seqs, high, HEAD_DIM), BF16),
            pltpu.VMEM((high, keys), F32),
            pltpu.VMEM((high, keys), BF16),
            pltpu.VMEM((2 * rows, HEAD_DIM), F32),
            pltpu.VMEM((high, HEAD_DIM), F32),
            pltpu.VMEM((2, tall, HEAD_DIM), F32),
            pltpu.VMEM((rows, seqs, wq.shape[1]), BF16),
            pltpu.VMEM((rows, HEAD_DIM), F32),
            pltpu.VMEM((rows, HEAD_DIM), F32),
            pltpu.VMEM((drafts, HEAD_DIM), F32),
            pltpu.VMEM((drafts, HEAD_DIM), F32),
            pltpu.VMEM((seqs, keys), jnp.int32),
            pltpu.VMEM((2, drafts, HEAD_DIM), BF16),
            pltpu.VMEM((seqs * G * steps, HEAD_DIM), F32),
            pltpu.VMEM((drafts, wq.shape[1]), F32),
            pltpu.VMEM(wo.shape, BF16),
            pltpu.VMEM((heads, drafts, wo.shape[1] // heads), F32),
            pltpu.VMEM((peers, drafts, wo.shape[1] // heads), F32),
            dma((8,)),
            dma((shards,)),
            dma((1,)),
            dma((8, 2, shards // 2)),
            dma((8, 2, shards // 2)),
            dma((2, shards // 2)),
            dma((2, shards // 2)),
            dma((peers,)),
            dma((peers,)),
        ],
        compiler_params=pltpu.CompilerParams(
            collective_id=0, has_side_effects=True, vmem_limit_bytes=60 * 1024 * 1024
        ),
    )(x, d, wq, wk, wv, wo, block_map, prompt_len, owner)


def solution(mesh):
    placed = (
        P("shard", "groups", None),
        P(None, "groups", "shard"),
        P("shard", ("head", "pair")),
        P("shard", ("head", "pair")),
        P("shard", ("head", "pair")),
        P(("head", "pair"), "shard"),
        P("groups"),
        P("groups"),
        P(("head", "pair"), "groups"),
    )
    return jax.shard_map(
        functools.partial(body, mesh.shape["shard"], mesh.shape["head"], mesh.shape["pair"]),
        mesh=mesh,
        in_specs=placed,
        out_specs=(
            P("shard", "groups", ("head", "pair")),
            P(None, ("groups", "shard"), ("head", "pair"), None),
            P(None, "groups", ("shard", "head", "pair")),
        ),
        check_vma=False,
    )
```

time: 312 us -> 271 us (0.87)
  Pallas kernels: 0 us -> 265 us
  waiting for transfers between devices: 157 us -> 0 us
  starting transfers between devices: 46.2 us -> 0 us
  local copies, waits for them, and re-layouts: 40 us -> 4.45 us
  matrix products: 35.3 us -> 0 us
  between operations: 19.7 us -> 0.64 us
  other arithmetic: 12.9 us -> 0 us
    pallas_call x0 -> x1, Pallas kernels: none -> 265 us  [body(): pl.pallas_call(functools.partial(kernel, shards, heads, pairs), out_shape...]
    all_gather x2 -> x0, waiting for transfers between devices: 157 us -> none  [in_one_piece(): out = lax.all_gather(both, axis, axis=dim, tiled=True)]
    all_to_all x3 -> x0, starting transfers between devices: 46.1 us -> none  [the longest x2 31.3 us: from_everyone(): lax.all_to_all(jnp.broadcast_to(shard[None], (devices, *shard.shape)), ax...]
    dot_general x10 -> x0, matrix products: 35.3 us -> none  [the longest x3 20.6 us: body(): jnp.dot(all_rows, piece, preferred_element_type=jnp.float32)]
    reshape x6 -> x0, local copies, waits for them, and re-layouts: 14.2 us -> none  [the longest x1 12.5 us: body(): prompt_tokens.reshape(local_rows * seqs, width)]
    unnamed x22 -> x2, local copies, waits for them, and re-layouts: 16 us -> 3.27 us
    reduce_sum x5 -> x0, other arithmetic: 4.51 us -> none  [the longest x1 3.59 us: body(): total = jnp.sum(weight, -1)]
    concatenate x3 -> x0, other arithmetic: 3.75 us -> none  [the longest x2 3.07 us: in_one_piece(): both = jnp.concatenate(arrays, axis=along)]
  transfers between devices with their start and end apart: 5 -> 0, of which waited for: 2 -> 0; matrix products, arithmetic and copies ran while one was open for 19% -> 0% of each run, Pallas kernels for 0% -> 0%
where the time goes in v1:
time: 271 us; the launch traced here: 270 us
  Pallas kernels  265 us (98%)
  local copies, waits for them, and re-layouts  4.45 us (2%)
    pallas_call x1, Pallas kernels, body(): pl.pallas_call(functools.partial(kernel, shards, heads, pairs), out_shape...  265 us

profile of v1, /device:TPU:33, one launch (start us, length us, event | category | flops | bytes accessed | tf_op | source)
XLA Modules:
  0.0 270.3 jit_solution(11661976442791872729)
XLA Ops:
  0.6 265.2 %shard_map.112 = (bf16[128,4,512]{2,1,0:T(4,128)(2,1)}, bf16[2,1,1,128]{3,2,1,0:T(2,128)(2,1)}, bf16[2,4,64]{2,1,0:T(4,128)(2,1)}) custom-call(bf16[128,4,8192]{2,1,0:T(4,128)(2,1)} %x_hbm.1, bf16[2,4,512]{2,1,0:T(4,128)(2,1)} %d_ref.1, bf16[512,512]{1,0:T(8,128)(2,1)} %wq_hbm.1, bf16[512,128]{1,0:T(8,128)(2,1)} %wk_hbm.1, bf16[512,128]{1,0:T(8,128)(2,1)} %wv_hbm.1, ...), custom_call_target="tpu_custom_call" | custom-call | tf_op jit(solution)/shard_map/pallas_call | solution.py:418
  265.8 1.2 copy.12
  267.0 2.0 copy.15
  269.0 1.3 copy.16

commit v2 on v1

v2 whole, which is shorter than its diff:
```python
import functools
import math

import jax
import jax.numpy as jnp
from jax import lax
from jax.experimental import pallas as pl
from jax.experimental.pallas import tpu as pltpu
from jax.sharding import PartitionSpec as P

HEAD_DIM = 128
G = 4
BLK = 64
NEG = -1e30
THETA = 500000.0
MESH = pl.DeviceIdType.MESH
F32 = jnp.float32
BF16 = jnp.bfloat16
FAR = 1 << 30
DRAFT_ROWS = 16

PHASES = ((0, 1), (2, 3, 4, 5), (6, 7))
EXTRA = (160, 160)
UNITS_A = {3: (0, 1), 4: (1, 2), 5: (2, 3), 6: (3, 4), 7: (4, 5), 8: (5, 6)}
LATE_A = {1: (6, 7), 2: (7, 8)}
CACHE_AT = 2
UNITS_B = {3: (0, 1), 4: (1, 2), 5: (2, 3), 6: (3, 4), 7: (4, 5), 8: (5, 6)}
LATE_B = {1: (6, 7), 2: (7, 8)}
QUERY_AT = 2
UNITS_C = {3: (0, 2), 4: (2, 4), 5: (4, 5), 6: (5, 6), 7: (6, 7), 8: (7, 8)}


def rope_tables(pos):
    lane = lax.broadcasted_iota(jnp.int32, (pos.shape[0], HEAD_DIM), 1)
    half = HEAD_DIM // 2
    pair = jnp.where(lane < half, lane, lane - half).astype(F32)
    freq = jnp.exp(pair * (-math.log(THETA) / half))
    angle = pos.astype(F32) * freq
    sine = jnp.sin(angle)
    return jnp.cos(angle), jnp.where(lane < half, -sine, sine)


def rope(v, cosine, sine):
    return v * cosine + pltpu.roll(v, HEAD_DIM // 2, 1) * sine


def bounds(table, s):
    if isinstance(s, int):
        return table.get(s, (0, 0))
    low, high = jnp.int32(0), jnp.int32(0)
    for k, (a, b) in table.items():
        low = jnp.where(s == k, a, low)
        high = jnp.where(s == k, b, high)
    return low, high


def over(table, s, f):
    low, high = bounds(table, s)
    if isinstance(s, int) and low == high:
        return

    def one(u, _):
        f(u)
        return 0

    lax.fori_loop(low, high, one, 0)


def kernel(
    groups, shards, heads, pairs,
    x_hbm, d_ref, wq_hbm, wk_hbm, wv_hbm, wo_hbm, map_ref, len_ref, owner_ref,
    out_hbm, dattn_ref, dec_ref,
    buf, xin, xs, dbuf, acc, qbuf, mbuf, lbuf, obuf, limit, ostage, oready, cosb, sinb, dcos, dsin, kpos,
    dkv, aflat, lhs, wo, part, parts,
    load_sem, x_sem, out_sem, send_sem, recv_sem, ysend_sem, yrecv_sem, dsend_sem, drecv_sem, psend_sem, precv_sem,
):
    me = lax.axis_index("shard")
    head = lax.axis_index("head")
    pair = lax.axis_index("pair")
    group = lax.axis_index("groups")
    right = lax.rem(me + 1, shards)
    left = lax.rem(me + shards - 1, shards)
    odd = lax.rem(group, 2)
    twin = group + 1 - 2 * odd
    far = shards // 2
    rows, seqs, width = x_hbm.shape
    depth = wq_hbm.shape[0]
    steps = d_ref.shape[0]
    tall = rows * seqs
    drafts = steps * seqs
    per = rows // BLK
    scale = 1.0 / math.sqrt(HEAD_DIM)
    factor = scale * math.log2(math.e)
    peers = heads * pairs
    place = head * pairs + pair
    high = G * rows + DRAFT_ROWS

    barrier = pltpu.get_barrier_semaphore()
    for z in (left, right):
        pl.semaphore_signal(barrier, inc=1, device_id={"shard": z}, device_id_type=MESH)
    pl.semaphore_signal(barrier, inc=1, device_id={"groups": twin}, device_id_type=MESH)
    for k in range(1, peers):
        other = lax.rem(place + k, peers)
        pl.semaphore_signal(
            barrier, inc=1, device_id={"head": other // pairs, "pair": other % pairs}, device_id_type=MESH
        )

    def owner_of(v):
        half = (v + 1) // 2
        return lax.rem(me + shards + jnp.where(lax.rem(v, 2) == 1, -half, half), shards)

    sources = [wk_hbm, wv_hbm] + [wq_hbm.at[:, g * HEAD_DIM : (g + 1) * HEAD_DIM] for g in range(G)]
    loads = [pltpu.make_async_copy(src, buf.at[s, me], load_sem.at[s]) for s, src in enumerate(sources)]
    wo_load = pltpu.make_async_copy(wo_hbm, wo, load_sem.at[6])

    def x_load(owner):
        return pltpu.make_async_copy(
            x_hbm.at[:, :, pl.ds(pl.multiple_of(owner * depth, depth), depth)], xin.at[owner], x_sem.at[owner]
        )

    for load in loads:
        load.start()

    def start_x(v, _):
        x_load(owner_of(v)).start()
        return 0

    lax.fori_loop(0, shards, start_x, 0)
    wo_load.start()

    d_all = d_ref[...].astype(F32)
    dbuf[me] = jnp.concatenate([d_all[t] for t in range(steps)], 0).astype(BF16)

    pl.semaphore_wait(barrier, 2 + 1 + peers - 1)

    def items(phase):
        if phase == 2:
            return [(0, 0, depth // 2), (1, depth // 2, depth // 2)]
        extra = EXTRA[phase]
        found = [(0, odd * (depth - extra), extra)]
        if 2 * extra < depth:
            found.append((1, extra, depth - 2 * extra))
        return found

    def hop(stream, item, way, s):
        index, first, count = item
        owner = lax.rem(me + shards - (s - 1), shards) if way == 0 else lax.rem(me + (s - 1), shards)
        if isinstance(s, int) and s == far:
            count = count // 2
            first = first + way * count
        if not isinstance(first, int):
            first = pl.multiple_of(first, 16)
        ref = buf.at[stream, owner, pl.ds(first, count)]
        lane = stream * 4 + index * 2 + way
        return pltpu.make_async_remote_copy(
            src_ref=ref, dst_ref=ref, send_sem=send_sem.at[lane], recv_sem=recv_sem.at[lane, s - 1],
            device_id={"shard": right if way == 0 else left}, device_id_type=MESH,
        )

    def hand(stream, v):
        extra = EXTRA[0 if stream in PHASES[0] else 1]
        ref = buf.at[stream, owner_of(v), pl.ds(pl.multiple_of(odd * (depth - extra), 16), extra)]
        return pltpu.make_async_remote_copy(
            src_ref=ref, dst_ref=ref, send_sem=ysend_sem.at[stream, v], recv_sem=yrecv_sem.at[stream, v],
            device_id={"groups": twin}, device_id_type=MESH,
        )

    def draft_hop(way, s):
        owner = lax.rem(me + shards - (s - 1), shards) if way == 0 else lax.rem(me + (s - 1), shards)
        return pltpu.make_async_remote_copy(
            src_ref=dbuf.at[owner], dst_ref=dbuf.at[owner], send_sem=dsend_sem.at[way],
            recv_sem=drecv_sem.at[way, s - 1], device_id={"shard": right if way == 0 else left}, device_id_type=MESH,
        )

    def launch(phase):
        for item in items(phase):
            for stream in PHASES[phase]:
                for way in range(2):
                    hop(stream, item, way, 1).start()
        if phase == 0:
            for way in range(2):
                draft_hop(way, 1).start()

    def pass_on(phase, s):
        for item in items(phase):
            for stream in PHASES[phase]:
                for way in range(2):
                    hop(stream, item, way, s).wait_recv()
                    hop(stream, item, way, s).wait_send()

                    @pl.when(s < far - 1)
                    def _():
                        hop(stream, item, way, s + 1).start()

                    @pl.when(s == far - 1)
                    def _():
                        hop(stream, item, way, far).start()

                    if phase < 2 and item[0] == 0:
                        hand(stream, 2 * s - 1 + way).start()
        if phase == 0:
            for way in range(2):
                draft_hop(way, s).wait_recv()
                draft_hop(way, s).wait_send()

            draft_hop(0, s + 1).start()

            @pl.when(s < far - 1)
            def _():
                draft_hop(1, s + 1).start()

    def finish(phase):
        for item in items(phase):
            for stream in PHASES[phase]:
                for way in range(2):
                    hop(stream, item, way, far).wait_recv()
                    hop(stream, item, way, far).wait_send()
                if phase < 2 and item[0] == 0:
                    hand(stream, 2 * far - 1).start()
        if phase == 0:
            draft_hop(0, far).wait_recv()
            draft_hop(0, far).wait_send()

    def ring(phase, work, ready_next):
        def step(s, _):
            pass_on(phase, s)
            work(s)
            return 0

        lax.fori_loop(1, far, step, 0)
        ready_next()
        finish(phase)
        work(far)

    def multiply(phase, u):
        streams = PHASES[phase]

        def one(v, _):
            owner = owner_of(v)
            if phase == 0:
                x_load(owner).wait()
                xs[owner, 0:tall] = xin[owner].reshape(tall, depth)
                xs[owner, tall : tall + drafts] = dbuf[owner]

            @pl.when(v > 0)
            def _():
                for stream in streams:
                    hand(stream, v).wait_recv()

            w = jnp.concatenate([buf[stream, owner] for stream in streams], 1)
            got = jnp.dot(xs[owner], w, preferred_element_type=F32)
            for k, stream in enumerate(streams):
                acc[stream] += got[:, k * HEAD_DIM : (k + 1) * HEAD_DIM]
            return 0

        lax.fori_loop(2 * u, 2 * u + 2, one, 0)

    def own_rows(count):
        row = lax.rem(lax.broadcasted_iota(jnp.int32, (count, 1), 0), rows)
        pos = row + map_ref[me * per] * BLK
        for j in range(1, per):
            pos = jnp.where(row >= j * BLK, row - j * BLK + map_ref[me * per + j] * BLK, pos)
        return pos

    loads[0].wait()
    loads[1].wait()
    launch(0)

    for stream in range(6):
        acc[stream] = jnp.zeros(acc.shape[1:], F32)
    cosb[...], sinb[...] = rope_tables(own_rows(rows))
    drow = lax.broadcasted_iota(jnp.int32, (drafts, 1), 0)
    dpos = jnp.zeros((drafts, 1), jnp.int32)
    for t in range(steps):
        for b in range(seqs):
            dpos = jnp.where(drow == t * seqs + b, len_ref[b] + t, dpos)
    dcos[...], dsin[...] = rope_tables(dpos)
    seq = lax.broadcasted_iota(jnp.int32, (seqs, rows), 0)
    lengths = jnp.zeros((seqs, rows), jnp.int32)
    for b in range(seqs):
        lengths = jnp.where(seq == b, len_ref[b], lengths)

    def positions(z, _):
        lane = lax.broadcasted_iota(jnp.int32, (seqs, rows), 1)
        where = lane + map_ref[z * per] * BLK
        for j in range(1, per):
            where = jnp.where(lane >= j * BLK, lane - j * BLK + map_ref[z * per + j] * BLK, where)
        kpos[z] = jnp.where(where < lengths, where, FAR)
        return 0

    lax.fori_loop(0, shards, positions, 0)
    limit[0 : G * rows] = jnp.broadcast_to(own_rows(G * rows), (G * rows, HEAD_DIM))
    limit[G * rows : high] = jnp.full((DRAFT_ROWS, HEAD_DIM), FAR - 1, jnp.int32)

    def next0():
        for load in loads[2:]:
            load.wait()
        launch(1)

    ring(0, lambda s: over(UNITS_A, s, functools.partial(multiply, 0)), next0)

    def own_cache():
        def one(b, _):
            k = acc[0, pl.ds(b, rows, stride=seqs), :]
            v = acc[1, pl.ds(b, rows, stride=seqs), :]
            at = pl.ds(pl.multiple_of(b * rows, rows), rows)
            buf[6, me, at] = rope(k, cosb[...], sinb[...]).astype(BF16)
            buf[7, me, at] = v.astype(BF16)
            return 0

        lax.fori_loop(0, seqs, one, 0)
        dkv[0] = rope(acc[0, tall : tall + drafts, :], dcos[...], dsin[...]).astype(BF16)
        dkv[1] = acc[1, tall : tall + drafts, :].astype(BF16)

    def work1(s):
        if not isinstance(s, int):
            over(LATE_A, s, functools.partial(multiply, 0))
            pl.when(s == CACHE_AT)(own_cache)
        over(UNITS_B, s, functools.partial(multiply, 1))

    ring(1, work1, lambda: launch(2))

    def queries():
        dq = [rope(acc[2 + g, tall : tall + drafts, :], dcos[...], dsin[...]) for g in range(G)]
        for b in range(seqs):
            pieces = [dq[g][t * seqs + b : t * seqs + b + 1] for g in range(G) for t in range(steps)]
            pieces.append(jnp.zeros((DRAFT_ROWS - G * steps, HEAD_DIM), F32))
            qbuf[b, G * rows : high] = jnp.concatenate(pieces, 0).astype(BF16)

        def one(b, _):
            for g in range(G):
                q = acc[2 + g, pl.ds(b, rows, stride=seqs), :]
                qbuf[b, g * rows : (g + 1) * rows] = rope(q, cosb[...], sinb[...]).astype(BF16)
            mbuf[b] = jnp.full((high, HEAD_DIM), NEG, F32)
            lbuf[b] = jnp.zeros((high, HEAD_DIM), F32)
            obuf[b] = jnp.zeros((high, HEAD_DIM), F32)
            return 0

        lax.fori_loop(0, seqs, one, 0)

    def attend(u):
        first, second = owner_of(2 * u), owner_of(2 * u + 1)

        def one(b, _):
            at = pl.ds(pl.multiple_of(b * rows, rows), rows)
            k = jnp.concatenate([buf[6, first, at, :], buf[6, second, at, :]], 0)
            v = jnp.concatenate([buf[7, first, at, :], buf[7, second, at, :]], 0)
            kp0 = kpos[first, pl.ds(b, 1), :]
            kp1 = kpos[second, pl.ds(b, 1), :]
            tile = high // 3
            for r in range(0, high, tile):
                at_r = slice(r, r + tile)
                s = lax.dot_general(qbuf[b, at_r], k, (((1,), (1,)), ((), ())), preferred_element_type=F32)
                most = limit[at_r]
                s0 = jnp.where(kp0 <= most, s[:, 0:rows], NEG)
                s1 = jnp.where(kp1 <= most, s[:, rows : 2 * rows], NEG)
                before = mbuf[b, at_r]
                top = jnp.maximum(before, jnp.max(jnp.maximum(s0, s1), 1, keepdims=True))
                shrink = jnp.exp2((before - top) * factor)
                w0 = jnp.exp2((s0 - top) * factor)
                w1 = jnp.exp2((s1 - top) * factor)
                mbuf[b, at_r] = top
                lbuf[b, at_r] = lbuf[b, at_r] * shrink + (w0 + w1)
                w = jnp.concatenate([w0, w1], 1).astype(BF16)
                obuf[b, at_r] = obuf[b, at_r] * shrink + jnp.dot(w, v, preferred_element_type=F32)
            return 0

        lax.fori_loop(0, seqs, one, 0)

    def work2(s):
        if not isinstance(s, int):
            over(LATE_B, s, functools.partial(multiply, 1))
            pl.when(s == QUERY_AT)(queries)
        over(UNITS_C, s, attend)

    ring(2, work2, lambda: None)

    wo_load.wait()
    r = lax.broadcasted_iota(jnp.int32, (DRAFT_ROWS, drafts), 0)
    c = lax.broadcasted_iota(jnp.int32, (DRAFT_ROWS, drafts), 1)
    for b in range(seqs):
        at_r = slice(G * rows, high)
        new = lax.dot_general(qbuf[b, at_r], dkv[0], (((1,), (1,)), ((), ())), preferred_element_type=F32)
        seen = (lax.rem(c, seqs) == b) & (c // seqs <= lax.rem(r, steps))
        new = jnp.where(seen, new, NEG)
        before = mbuf[b, at_r][:, 0:1]
        top = jnp.maximum(before, jnp.max(new, 1, keepdims=True))
        shrink = jnp.exp2((before - top) * factor)
        w = jnp.where(seen, jnp.exp2((new - top) * factor), 0.0)
        total = jnp.sum(lbuf[b, at_r], 1, keepdims=True) * shrink + jnp.sum(w, 1, keepdims=True)
        mixed = obuf[b, at_r] * shrink + jnp.dot(w.astype(BF16), dkv[1], preferred_element_type=F32)
        attn = (mixed / total).astype(BF16).astype(F32)
        aflat[b * G * steps : (b + 1) * G * steps] = attn[0 : G * steps]
    for g in range(G):
        for t in range(steps):
            lhs[t * seqs : (t + 1) * seqs, g * HEAD_DIM : (g + 1) * HEAD_DIM] = aflat[
                pl.ds(g * steps + t, seqs, stride=G * steps), :
            ]
    partial = jnp.dot(lhs[...].astype(BF16), wo[...], preferred_element_type=F32)
    wide = partial.shape[1] // heads
    for h in range(heads):
        part[h] = partial[:, h * wide : (h + 1) * wide]
    parts[place] = part[head]

    def give(k):
        other = lax.rem(place + k, peers)
        return pltpu.make_async_remote_copy(
            src_ref=part.at[other // pairs], dst_ref=parts.at[place], send_sem=psend_sem.at[k], recv_sem=precv_sem.at[k],
            device_id={"head": other // pairs, "pair": other % pairs}, device_id_type=MESH,
        )

    r1 = lax.broadcasted_iota(jnp.int32, (seqs * G * steps, 1), 0)
    mine = jnp.zeros((seqs * G * steps, 1), jnp.int32)
    for p in range(seqs * G):
        mine = jnp.where(r1 // steps == p, owner_ref[0, p], mine)
    picked = jnp.where(mine == me, aflat[...], 0.0)
    for t in range(steps):
        dattn_ref[t, 0] = jnp.sum(
            jnp.where(lax.rem(r1, steps) == t, picked, 0.0), 0, keepdims=True
        ).astype(BF16)

    for k in range(1, peers):
        give(k).start()

    def put(b, _):
        for g in range(G):
            at_g = slice(g * rows, (g + 1) * rows)
            total = jnp.sum(lbuf[b, at_g], 1, keepdims=True)
            ostage[g, pl.ds(b, rows, stride=seqs), :] = obuf[b, at_g] / total
        return 0

    lax.fori_loop(0, seqs, put, 0)
    for g in range(G):
        oready[:, :, g * HEAD_DIM : (g + 1) * HEAD_DIM] = ostage[g].astype(BF16).reshape(rows, seqs, HEAD_DIM)
    store = pltpu.make_async_copy(oready, out_hbm, out_sem.at[0])
    store.start()

    for k in range(1, peers):
        give(k).wait_recv()
    summed = jnp.sum(parts[...], 0)
    narrow = wide // pairs
    got = summed[:, 0:narrow]
    for j in range(1, pairs):
        got = jnp.where(pair == j, summed[:, j * narrow : (j + 1) * narrow], got)
    for t in range(steps):
        dec_ref[t] = got[t * seqs : (t + 1) * seqs].astype(BF16)

    for k in range(1, peers):
        give(k).wait_send()

    def drain(v, _):
        for stream in range(6):
            hand(stream, v).wait_send()
        return 0

    lax.fori_loop(1, shards, drain, 0)
    store.wait()


def body(groups, shards, heads, pairs, x, d, wq, wk, wv, wo, block_map, prompt_len, owner):
    rows, seqs, width = x.shape
    depth = wq.shape[0]
    steps = d.shape[0]
    drafts = steps * seqs
    tall = rows * seqs
    peers = heads * pairs
    high = G * rows + DRAFT_ROWS
    any_ = pl.BlockSpec(memory_space=pl.ANY)
    vmem = pl.BlockSpec(memory_space=pltpu.VMEM)
    smem = pl.BlockSpec(memory_space=pltpu.SMEM)
    dma = pltpu.SemaphoreType.DMA
    return pl.pallas_call(
        functools.partial(kernel, groups, shards, heads, pairs),
        out_shape=(
            jax.ShapeDtypeStruct((rows, seqs, wq.shape[1]), BF16),
            jax.ShapeDtypeStruct((steps, 1, 1, HEAD_DIM), BF16),
            jax.ShapeDtypeStruct((steps, seqs, wo.shape[1] // peers), BF16),
        ),
        in_specs=[any_, vmem, any_, any_, any_, any_, smem, smem, smem],
        out_specs=(any_, vmem, vmem),
        scratch_shapes=[
            pltpu.VMEM((8, shards, depth, HEAD_DIM), BF16),
            pltpu.VMEM((shards, rows, seqs, depth), BF16),
            pltpu.VMEM((shards, tall + drafts, depth), BF16),
            pltpu.VMEM((shards, drafts, depth), BF16),
            pltpu.VMEM((6, tall + drafts, HEAD_DIM), F32),
            pltpu.VMEM((seqs, high, HEAD_DIM), BF16),
            pltpu.VMEM((seqs, high, HEAD_DIM), F32),
            pltpu.VMEM((seqs, high, HEAD_DIM), F32),
            pltpu.VMEM((seqs, high, HEAD_DIM), F32),
            pltpu.VMEM((high, HEAD_DIM), jnp.int32),
            pltpu.VMEM((G, tall, HEAD_DIM), F32),
            pltpu.VMEM((rows, seqs, wq.shape[1]), BF16),
            pltpu.VMEM((rows, HEAD_DIM), F32),
            pltpu.VMEM((rows, HEAD_DIM), F32),
            pltpu.VMEM((drafts, HEAD_DIM), F32),
            pltpu.VMEM((drafts, HEAD_DIM), F32),
            pltpu.VMEM((shards, seqs, rows), jnp.int32),
            pltpu.VMEM((2, drafts, HEAD_DIM), BF16),
            pltpu.VMEM((seqs * G * steps, HEAD_DIM), F32),
            pltpu.VMEM((drafts, wq.shape[1]), F32),
            pltpu.VMEM(wo.shape, BF16),
            pltpu.VMEM((heads, drafts, wo.shape[1] // heads), F32),
            pltpu.VMEM((peers, drafts, wo.shape[1] // heads), F32),
            dma((7,)),
            dma((shards,)),
            dma((1,)),
            dma((32,)),
            dma((32, shards // 2)),
            dma((6, shards)),
            dma((6, shards)),
            dma((2,)),
            dma((2, shards // 2)),
            dma((peers,)),
            dma((peers,)),
        ],
        compiler_params=pltpu.CompilerParams(
            collective_id=0, has_side_effects=True, vmem_limit_bytes=60 * 1024 * 1024
        ),
    )(x, d, wq, wk, wv, wo, block_map, prompt_len, owner)


def solution(mesh):
    placed = (
        P("shard", "groups", None),
        P(None, "groups", "shard"),
        P("shard", ("head", "pair")),
        P("shard", ("head", "pair")),
        P("shard", ("head", "pair")),
        P(("head", "pair"), "shard"),
        P("groups"),
        P("groups"),
        P(("head", "pair"), "groups"),
    )
    sizes = [mesh.shape[name] for name in ("groups", "shard", "head", "pair")]
    return jax.shard_map(
        functools.partial(body, *sizes),
        mesh=mesh,
        in_specs=placed,
        out_specs=(
            P("shard", "groups", ("head", "pair")),
            P(None, ("groups", "shard"), ("head", "pair"), None),
            P(None, "groups", ("shard", "head", "pair")),
        ),
        check_vma=False,
    )
```

time: 271 us -> 183 us (0.68)
  Pallas kernels: 265 us -> 178 us
    pallas_call x1, Pallas kernels: 265 us -> 178 us  [body(): pl.pallas_call(functools.partial(kernel, groups, shards, heads, pairs), o...]
where the time goes in v2:
time: 183 us
  Pallas kernels  178 us (97%)
  local copies, waits for them, and re-layouts  4.45 us (2%)
    pallas_call x1, Pallas kernels, body(): pl.pallas_call(functools.partial(kernel, groups, shards, heads, pairs), o...  178 us

profile of v2, /device:TPU:33, one launch (start us, length us, event | category | flops | bytes accessed | tf_op | source)
XLA Modules:
  0.0 182.7 jit_solution(14368668937962590735)
XLA Ops:
  0.6 177.6 %shard_map.112 = (bf16[128,4,512]{2,1,0:T(4,128)(2,1)}, bf16[2,1,1,128]{3,2,1,0:T(2,128)(2,1)}, bf16[2,4,64]{2,1,0:T(4,128)(2,1)}) custom-call(bf16[128,4,8192]{2,1,0:T(4,128)(2,1)} %x_hbm.1, bf16[2,4,512]{2,1,0:T(4,128)(2,1)} %d_ref.1, bf16[512,512]{1,0:T(8,128)(2,1)} %wq_hbm.1, bf16[512,128]{1,0:T(8,128)(2,1)} %wk_hbm.1, bf16[512,128]{1,0:T(8,128)(2,1)} %wv_hbm.1, ...), custom_call_target="tpu_custom_call" | custom-call | tf_op jit(solution)/shard_map/pallas_call | solution.py:472
  178.3 1.2 copy.12
  179.5 2.0 %copy.15 = bf16[128,4,512]{2,1,0:T(4,128)(2,1)} copy(bf16[128,4,512]{2,1,0:T(4,128)(2,1)} %get-tuple-element.9) | data formatting | bytes 1048576
  181.5 1.3 copy.16

commit v3 on v2

--- a/solution.py
+++ b/solution.py
@@ -20,14 +20,17 @@
 DRAFT_ROWS = 16
 
 PHASES = ((0, 1), (2, 3, 4, 5), (6, 7))
-EXTRA = (160, 160)
+EXTRA = (176, 208)
+PARTS = (((0, 1, True), (1, 1, True), (0, 1, False), (1, 1, False)), ((2, 2, True), (4, 2, True), (2, 4, False)))
+LANES = (0, 8, 0)
+TURNS = 4
 UNITS_A = {3: (0, 1), 4: (1, 2), 5: (2, 3), 6: (3, 4), 7: (4, 5), 8: (5, 6)}
 LATE_A = {1: (6, 7), 2: (7, 8)}
 CACHE_AT = 2
-UNITS_B = {3: (0, 1), 4: (1, 2), 5: (2, 3), 6: (3, 4), 7: (4, 5), 8: (5, 6)}
-LATE_B = {1: (6, 7), 2: (7, 8)}
-QUERY_AT = 2
-UNITS_C = {3: (0, 2), 4: (2, 4), 5: (4, 5), 6: (5, 6), 7: (6, 7), 8: (7, 8)}
+UNITS_B = {3: (0, 1), 4: (1, 2), 5: (2, 3), 6: (3, 4), 8: (4, 5)}
+LATE_B = {1: (5, 6), 3: (6, 7), 4: (7, 8)}
+QUERY_AT = 4
+UNITS_C = {4: (0, 1), 5: (1, 3), 6: (3, 5), 7: (5, 7)}
 
 
 def rope_tables(pos):
@@ -133,35 +136,41 @@
 
     pl.semaphore_wait(barrier, 2 + 1 + peers - 1)
 
-    def items(phase):
+    def pieces(phase):
         if phase == 2:
-            return [(0, 0, depth // 2), (1, depth // 2, depth // 2)]
-        extra = EXTRA[phase]
-        found = [(0, odd * (depth - extra), extra)]
-        if 2 * extra < depth:
-            found.append((1, extra, depth - 2 * extra))
-        return found
-
-    def hop(stream, item, way, s):
-        index, first, count = item
+            found = [(6 + k % 2, 1, k // 2 * (depth // 2), depth // 2, False) for k in range(4)]
+        else:
+            extra = EXTRA[phase]
+            found = [
+                (stream, count, odd * (depth - extra), extra, True) if own else (stream, count, extra, depth - 2 * extra, False)
+                for stream, count, own in PARTS[phase]
+            ]
+        return [(LANES[phase] + 2 * k, *piece) for k, piece in enumerate(found)]
+
+    def hop(piece, way, s):
+        lane, stream, streams, first, count, _ = piece
         owner = lax.rem(me + shards - (s - 1), shards) if way == 0 else lax.rem(me + (s - 1), shards)
         if isinstance(s, int) and s == far:
-            count = count // 2
-            first = first + way * count
+            upper = (count // 2 + 15) // 16 * 16
+            first = first + way * upper
+            count = count - upper if way else upper
         if not isinstance(first, int):
             first = pl.multiple_of(first, 16)
-        ref = buf.at[stream, owner, pl.ds(first, count)]
-        lane = stream * 4 + index * 2 + way
+        ref = buf.at[pl.ds(stream, streams), owner, pl.ds(first, count)]
+        turn = (s - 1) % TURNS if isinstance(s, int) else lax.rem(s - 1, TURNS)
         return pltpu.make_async_remote_copy(
-            src_ref=ref, dst_ref=ref, send_sem=send_sem.at[lane], recv_sem=recv_sem.at[lane, s - 1],
+            src_ref=ref, dst_ref=ref, send_sem=send_sem.at[lane + way], recv_sem=recv_sem.at[lane + way, turn],
             device_id={"shard": right if way == 0 else left}, device_id_type=MESH,
         )
 
-    def hand(stream, v):
-        extra = EXTRA[0 if stream in PHASES[0] else 1]
-        ref = buf.at[stream, owner_of(v), pl.ds(pl.multiple_of(odd * (depth - extra), 16), extra)]
+    def hand(phase, v):
+        extra = EXTRA[phase]
+        streams = PHASES[phase]
+        ref = buf.at[
+            pl.ds(streams[0], len(streams)), owner_of(v), pl.ds(pl.multiple_of(odd * (depth - extra), 16), extra)
+        ]
         return pltpu.make_async_remote_copy(
-            src_ref=ref, dst_ref=ref, send_sem=ysend_sem.at[stream, v], recv_sem=yrecv_sem.at[stream, v],
+            src_ref=ref, dst_ref=ref, send_sem=ysend_sem.at[phase, v], recv_sem=yrecv_sem.at[phase, v],
             device_id={"groups": twin}, device_id_type=MESH,
         )
 
@@ -173,31 +182,31 @@
         )
 
     def launch(phase):
-        for item in items(phase):
-            for stream in PHASES[phase]:
-                for way in range(2):
-                    hop(stream, item, way, 1).start()
+        for piece in pieces(phase):
+            for way in range(2):
+                hop(piece, way, 1).start()
         if phase == 0:
             for way in range(2):
                 draft_hop(way, 1).start()
 
     def pass_on(phase, s):
-        for item in items(phase):
-            for stream in PHASES[phase]:
-                for way in range(2):
-                    hop(stream, item, way, s).wait_recv()
-                    hop(stream, item, way, s).wait_send()
-
-                    @pl.when(s < far - 1)
-                    def _():
-                        hop(stream, item, way, s + 1).start()
-
-                    @pl.when(s == far - 1)
-                    def _():
-                        hop(stream, item, way, far).start()
-
-                    if phase < 2 and item[0] == 0:
-                        hand(stream, 2 * s - 1 + way).start()
+        found = pieces(phase)
+        owns = sum(piece[-1] for piece in found)
+        for k, piece in enumerate(found):
+            for way in range(2):
+                hop(piece, way, s).wait_recv()
+                hop(piece, way, s).wait_send()
+
+                @pl.when(s < far - 1)
+                def _():
+                    hop(piece, way, s + 1).start()
+
+                @pl.when(s == far - 1)
+                def _():
+                    hop(piece, way, far).start()
+
+                if k == owns - 1:
+                    hand(phase, 2 * s - 1 + way).start()
         if phase == 0:
             for way in range(2):
                 draft_hop(way, s).wait_recv()
@@ -210,13 +219,14 @@
                 draft_hop(1, s + 1).start()
 
     def finish(phase):
-        for item in items(phase):
-            for stream in PHASES[phase]:
-                for way in range(2):
-                    hop(stream, item, way, far).wait_recv()
-                    hop(stream, item, way, far).wait_send()
-                if phase < 2 and item[0] == 0:
-                    hand(stream, 2 * far - 1).start()
+        found = pieces(phase)
+        owns = sum(piece[-1] for piece in found)
+        for k, piece in enumerate(found):
+            for way in range(2):
+                hop(piece, way, far).wait_recv()
+                hop(piece, way, far).wait_send()
+            if k == owns - 1:
+                hand(phase, 2 * far - 1).start()
         if phase == 0:
             draft_hop(0, far).wait_recv()
             draft_hop(0, far).wait_send()
@@ -244,8 +254,7 @@
 
             @pl.when(v > 0)
             def _():
-                for stream in streams:
-                    hand(stream, v).wait_recv()
+                hand(phase, v).wait_recv()
 
             w = jnp.concatenate([buf[stream, owner] for stream in streams], 1)
             got = jnp.dot(xs[owner], w, preferred_element_type=F32)
@@ -338,7 +347,7 @@
 
         lax.fori_loop(0, seqs, one, 0)
 
-    def attend(u):
+    def attend(u, tiles=((0, high // 3), (high // 3, high // 3 * 2), (high // 3 * 2, high))):
         first, second = owner_of(2 * u), owner_of(2 * u + 1)
 
         def one(b, _):
@@ -347,9 +356,8 @@
             v = jnp.concatenate([buf[7, first, at, :], buf[7, second, at, :]], 0)
             kp0 = kpos[first, pl.ds(b, 1), :]
             kp1 = kpos[second, pl.ds(b, 1), :]
-            tile = high // 3
-            for r in range(0, high, tile):
-                at_r = slice(r, r + tile)
+            for low, end in tiles:
+                at_r = slice(low, end)
                 s = lax.dot_general(qbuf[b, at_r], k, (((1,), (1,)), ((), ())), preferred_element_type=F32)
                 most = limit[at_r]
                 s0 = jnp.where(kp0 <= most, s[:, 0:rows], NEG)
@@ -375,6 +383,7 @@
 
     ring(2, work2, lambda: None)
 
+    attend(far - 1, ((G * rows, high),))
     wo_load.wait()
     r = lax.broadcasted_iota(jnp.int32, (DRAFT_ROWS, drafts), 0)
     c = lax.broadcasted_iota(jnp.int32, (DRAFT_ROWS, drafts), 1)
@@ -414,13 +423,13 @@
     for p in range(seqs * G):
         mine = jnp.where(r1 // steps == p, owner_ref[0, p], mine)
     picked = jnp.where(mine == me, aflat[...], 0.0)
-    for t in range(steps):
-        dattn_ref[t, 0] = jnp.sum(
-            jnp.where(lax.rem(r1, steps) == t, picked, 0.0), 0, keepdims=True
-        ).astype(BF16)
+    found = [jnp.sum(jnp.where(lax.rem(r1, steps) == t, picked, 0.0), 0, keepdims=True) for t in range(steps)]
+    dattn_ref[0, 0] = jnp.concatenate(found, 0).astype(BF16)
 
     for k in range(1, peers):
         give(k).start()
+
+    attend(far - 1, ((0, 2 * rows), (2 * rows, 4 * rows)))
 
     def put(b, _):
         for g in range(G):
@@ -449,12 +458,17 @@
         give(k).wait_send()
 
     def drain(v, _):
-        for stream in range(6):
-            hand(stream, v).wait_send()
+        for phase in range(2):
+            hand(phase, v).wait_send()
         return 0
 
     lax.fori_loop(1, shards, drain, 0)
     store.wait()
+
+
+def settle(*refs):
+    for k in range(3):
+        refs[3 + k][...] = refs[k][...]
 
 
 def body(groups, shards, heads, pairs, x, d, wq, wk, wv, wo, block_map, prompt_len, owner):
@@ -469,11 +483,11 @@
     vmem = pl.BlockSpec(memory_space=pltpu.VMEM)
     smem = pl.BlockSpec(memory_space=pltpu.SMEM)
     dma = pltpu.SemaphoreType.DMA
-    return pl.pallas_call(
+    made = pl.pallas_call(
         functools.partial(kernel, groups, shards, heads, pairs),
         out_shape=(
             jax.ShapeDtypeStruct((rows, seqs, wq.shape[1]), BF16),
-            jax.ShapeDtypeStruct((steps, 1, 1, HEAD_DIM), BF16),
+            jax.ShapeDtypeStruct((1, 1, steps, HEAD_DIM), BF16),
             jax.ShapeDtypeStruct((steps, seqs, wo.shape[1] // peers), BF16),
         ),
         in_specs=[any_, vmem, any_, any_, any_, any_, smem, smem, smem],
@@ -505,10 +519,10 @@
             dma((7,)),
             dma((shards,)),
             dma((1,)),
-            dma((32,)),
-            dma((32, shards // 2)),
-            dma((6, shards)),
-            dma((6, shards)),
+            dma((14,)),
+            dma((14, TURNS)),
+            dma((2, shards)),
+            dma((2, shards)),
             dma((2,)),
             dma((2, shards // 2)),
             dma((peers,)),
@@ -518,6 +532,13 @@
             collective_id=0, has_side_effects=True, vmem_limit_bytes=60 * 1024 * 1024
         ),
     )(x, d, wq, wk, wv, wo, block_map, prompt_len, owner)
+    prefill, draft, decode = pl.pallas_call(
+        settle,
+        out_shape=tuple(jax.ShapeDtypeStruct(a.shape, a.dtype) for a in made),
+        in_specs=[vmem] * 3,
+        out_specs=(vmem,) * 3,
+    )(*made)
+    return prefill, draft.transpose(2, 0, 1, 3), decode
 
 
 def solution(mesh):

time: 183 us -> 169 us (0.923)
  Pallas kernels: 178 us -> 168 us
  local copies, waits for them, and re-layouts: 4.45 us -> 0 us
    pallas_call x1, Pallas kernels: 178 us -> 166 us  [body(): pl.pallas_call(functools.partial(kernel, groups, shards, heads, pairs), o...]
    unnamed x2 -> x0, local copies, waits for them, and re-layouts: 3.27 us -> none
    pallas_call x0 -> x1, Pallas kernels: none -> 1.88 us  [body(): pl.pallas_call(settle, out_shape=tuple((jax.ShapeDtypeStruct(a.shape, a.d...]
where the time goes in v3:
time: 169 us
  Pallas kernels  168 us (99%)
    pallas_call x1, Pallas kernels, body(): pl.pallas_call(functools.partial(kernel, groups, shards, heads, pairs), o...  166 us

profile of v3, /device:TPU:33, one launch (start us, length us, event | category | flops | bytes accessed | tf_op | source)
XLA Modules:
  0.0 169.0 jit_solution(11737579369503175873)
XLA Ops:
  0.6 166.5 %shard_map.112 = (bf16[128,4,512]{2,1,0:T(4,128)(2,1)}, bf16[1,1,2,128]{3,2,1,0:T(2,128)(2,1)}, bf16[2,4,64]{2,1,0:T(4,128)(2,1)}) custom-call(bf16[128,4,8192]{2,1,0:T(4,128)(2,1)} %x_hbm.1, bf16[2,4,512]{2,1,0:T(4,128)(2,1)} %d_ref.1, bf16[512,512]{1,0:T(8,128)(2,1)} %wq_hbm.1, bf16[512,128]{1,0:T(8,128)(2,1)} %wk_hbm.1, bf16[512,128]{1,0:T(8,128)(2,1)} %wv_hbm.1, ...), custom_call_target="tpu_custom_call" | custom-call | tf_op jit(solution)/shard_map/pallas_call | solution.py:486
  167.1 1.9 %shard_map.113 = (bf16[128,4,512]{2,1,0:T(4,128)(2,1)}, bf16[1,1,2,128]{3,2,1,0:T(2,128)(2,1)}, bf16[2,4,64]{2,1,0:T(4,128)(2,1)}) custom-call(bf16[128,4,512]{2,1,0:T(4,128)(2,1)} %get-tuple-element.9.refs_0_, bf16[1,1,2,128]{3,2,1,0:T(2,128)(2,1)} %get-tuple-element.10.refs_1_, bf16[2,4,64]{2,1,0:T(4,128)(2,1)} %get-tuple-element.11.refs_2_), custom_call_target="tpu_custom_call" | custom-call | tf_op jit(solution)/shard_map/pallas_call | solution.py:535

commit v4 on v3

--- a/solution.py
+++ b/solution.py
@@ -24,13 +24,12 @@
 PARTS = (((0, 1, True), (1, 1, True), (0, 1, False), (1, 1, False)), ((2, 2, True), (4, 2, True), (2, 4, False)))
 LANES = (0, 8, 0)
 TURNS = 4
-UNITS_A = {3: (0, 1), 4: (1, 2), 5: (2, 3), 6: (3, 4), 7: (4, 5), 8: (5, 6)}
-LATE_A = {1: (6, 7), 2: (7, 8)}
-CACHE_AT = 2
-UNITS_B = {3: (0, 1), 4: (1, 2), 5: (2, 3), 6: (3, 4), 8: (4, 5)}
-LATE_B = {1: (5, 6), 3: (6, 7), 4: (7, 8)}
-QUERY_AT = 4
-UNITS_C = {4: (0, 1), 5: (1, 3), 6: (3, 5), 7: (5, 7)}
+ORDER = (
+    "A1", "launchB", "A2", "B1", "a0", "A3", "a1", "A4", "B2", "a2", "b0", "A5", "a3", "A6", "B3", "a4", "b1",
+    "A7", "A8", "a5", "B4", "B5", "a6", "a7", "cache", "launchC", "b2", "B6", "C1", "b3", "B7", "C2", "b4",
+    "B8", "C3", "b5", "C4", "b6", "C5", "b7", "queries", "c0", "C6", "c1", "c2", "c3", "C7", "c4", "c5", "C8",
+    "c6",
+)
 
 
 def rope_tables(pos):
@@ -45,28 +44,6 @@
 
 def rope(v, cosine, sine):
     return v * cosine + pltpu.roll(v, HEAD_DIM // 2, 1) * sine
-
-
-def bounds(table, s):
-    if isinstance(s, int):
-        return table.get(s, (0, 0))
-    low, high = jnp.int32(0), jnp.int32(0)
-    for k, (a, b) in table.items():
-        low = jnp.where(s == k, a, low)
-        high = jnp.where(s == k, b, high)
-    return low, high
-
-
-def over(table, s, f):
-    low, high = bounds(table, s)
-    if isinstance(s, int) and low == high:
-        return
-
-    def one(u, _):
-        f(u)
-        return 0
-
-    lax.fori_loop(low, high, one, 0)
 
 
 def kernel(
@@ -197,14 +174,7 @@
                 hop(piece, way, s).wait_recv()
                 hop(piece, way, s).wait_send()
 
-                @pl.when(s < far - 1)
-                def _():
-                    hop(piece, way, s + 1).start()
-
-                @pl.when(s == far - 1)
-                def _():
-                    hop(piece, way, far).start()
-
+                hop(piece, way, s + 1).start()
                 if k == owns - 1:
                     hand(phase, 2 * s - 1 + way).start()
         if phase == 0:
@@ -212,11 +182,8 @@
                 draft_hop(way, s).wait_recv()
                 draft_hop(way, s).wait_send()
 
-            draft_hop(0, s + 1).start()
-
-            @pl.when(s < far - 1)
-            def _():
-                draft_hop(1, s + 1).start()
+                if s + 1 < far or way == 0:
+                    draft_hop(way, s + 1).start()
 
     def finish(phase):
         found = pieces(phase)
@@ -230,17 +197,6 @@
         if phase == 0:
             draft_hop(0, far).wait_recv()
             draft_hop(0, far).wait_send()
-
-    def ring(phase, work, ready_next):
-        def step(s, _):
-            pass_on(phase, s)
-            work(s)
-            return 0
-
-        lax.fori_loop(1, far, step, 0)
-        ready_next()
-        finish(phase)
-        work(far)
 
     def multiply(phase, u):
         streams = PHASES[phase]
@@ -301,12 +257,8 @@
     limit[0 : G * rows] = jnp.broadcast_to(own_rows(G * rows), (G * rows, HEAD_DIM))
     limit[G * rows : high] = jnp.full((DRAFT_ROWS, HEAD_DIM), FAR - 1, jnp.int32)
 
-    def next0():
-        for load in loads[2:]:
-            load.wait()
-        launch(1)
-
-    ring(0, lambda s: over(UNITS_A, s, functools.partial(multiply, 0)), next0)
+    for load in loads[2:]:
+        load.wait()
 
     def own_cache():
         def one(b, _):
@@ -320,14 +272,6 @@
         lax.fori_loop(0, seqs, one, 0)
         dkv[0] = rope(acc[0, tall : tall + drafts, :], dcos[...], dsin[...]).astype(BF16)
         dkv[1] = acc[1, tall : tall + drafts, :].astype(BF16)
-
-    def work1(s):
-        if not isinstance(s, int):
-            over(LATE_A, s, functools.partial(multiply, 0))
-            pl.when(s == CACHE_AT)(own_cache)
-        over(UNITS_B, s, functools.partial(multiply, 1))
-
-    ring(1, work1, lambda: launch(2))
 
     def queries():
         dq = [rope(acc[2 + g, tall : tall + drafts, :], dcos[...], dsin[...]) for g in range(G)]
@@ -375,13 +319,20 @@
 
         lax.fori_loop(0, seqs, one, 0)
 
-    def work2(s):
-        if not isinstance(s, int):
-            over(LATE_B, s, functools.partial(multiply, 1))
-            pl.when(s == QUERY_AT)(queries)
-        over(UNITS_C, s, attend)
-
-    ring(2, work2, lambda: None)
+    for word in ORDER:
+        if word == "cache":
+            own_cache()
+        elif word == "queries":
+            queries()
+        elif word.startswith("launch"):
+            launch("ABC".index(word[-1]))
+        elif word[0] == "c":
+            attend(int(word[1:]))
+        elif word[0] in "ab":
+            multiply("ab".index(word[0]), int(word[1:]))
+        else:
+            phase, s = "ABC".index(word[0]), int(word[1:])
+            (finish if s == far else lambda p: pass_on(p, s))(phase)
 
     attend(far - 1, ((G * rows, high),))
     wo_load.wait()

time: 169 us -> 173 us (1.024)
  Pallas kernels: 168 us -> 172 us
    pallas_call x1, Pallas kernels: 166 us -> 170 us  [body(): pl.pallas_call(functools.partial(kernel, groups, shards, heads, pairs), o...]
where the time goes in v4:
time: 173 us; the launch traced here: 172 us
  Pallas kernels  172 us (99%)
    pallas_call x1, Pallas kernels, body(): pl.pallas_call(functools.partial(kernel, groups, shards, heads, pairs), o...  170 us

profile of v4, /device:TPU:33, one launch (start us, length us, event | category | flops | bytes accessed | tf_op | source)
XLA Modules:
  0.0 172.5 jit_solution(5431413227142900700)
XLA Ops:
  0.6 170.0 %shard_map.112 = (bf16[128,4,512]{2,1,0:T(4,128)(2,1)}, bf16[1,1,2,128]{3,2,1,0:T(2,128)(2,1)}, bf16[2,4,64]{2,1,0:T(4,128)(2,1)}) custom-call(bf16[128,4,8192]{2,1,0:T(4,128)(2,1)} %x_hbm.1, bf16[2,4,512]{2,1,0:T(4,128)(2,1)} %d_ref.1, bf16[512,512]{1,0:T(8,128)(2,1)} %wq_hbm.1, bf16[512,128]{1,0:T(8,128)(2,1)} %wk_hbm.1, bf16[512,128]{1,0:T(8,128)(2,1)} %wv_hbm.1, ...), custom_call_target="tpu_custom_call" | custom-call | tf_op jit(solution)/shard_map/pallas_call | solution.py:437
  170.6 1.9 %shard_map.113 = (bf16[128,4,512]{2,1,0:T(4,128)(2,1)}, bf16[1,1,2,128]{3,2,1,0:T(2,128)(2,1)}, bf16[2,4,64]{2,1,0:T(4,128)(2,1)}) custom-call(bf16[128,4,512]{2,1,0:T(4,128)(2,1)} %get-tuple-element.9.refs_0_, bf16[1,1,2,128]{3,2,1,0:T(2,128)(2,1)} %get-tuple-element.10.refs_1_, bf16[2,4,64]{2,1,0:T(4,128)(2,1)} %get-tuple-element.11.refs_2_), custom_call_target="tpu_custom_call" | custom-call | tf_op jit(solution)/shard_map/pallas_call | solution.py:486

commit v5 on v3

--- a/solution.py
+++ b/solution.py
@@ -19,18 +19,23 @@
 FAR = 1 << 30
 DRAFT_ROWS = 16
 
-PHASES = ((0, 1), (2, 3, 4, 5), (6, 7))
+GROUPS = ((0, 1), (2, 3, 4, 5))
 EXTRA = (176, 208)
-PARTS = (((0, 1, True), (1, 1, True), (0, 1, False), (1, 1, False)), ((2, 2, True), (4, 2, True), (2, 4, False)))
-LANES = (0, 8, 0)
+PARTS = (
+    ((0, 1, True), (1, 1, True), (2, 1, True), (0, 1, False), (1, 1, False)),
+    ((3, 1, True), (4, 1, True), (5, 1, True), (2, 2, False), (4, 2, False)),
+)
+HANDS = ((0, 1, 0, 2), (0, 2, 2, 1), (1, 2, 3, 3))
+NEEDS = ((0,), (1, 2))
+LANES = (0, 10, 0)
 TURNS = 4
-UNITS_A = {3: (0, 1), 4: (1, 2), 5: (2, 3), 6: (3, 4), 7: (4, 5), 8: (5, 6)}
-LATE_A = {1: (6, 7), 2: (7, 8)}
-CACHE_AT = 2
-UNITS_B = {3: (0, 1), 4: (1, 2), 5: (2, 3), 6: (3, 4), 8: (4, 5)}
-LATE_B = {1: (5, 6), 3: (6, 7), 4: (7, 8)}
+UNITS_A = {2: (0, 1), 3: (1, 2), 4: (2, 3), 6: (3, 4), 7: (4, 5), 8: (5, 6)}
+LATE_A = {1: (6, 7), 3: (7, 8)}
+CACHE_AT = 3
+UNITS_B = {4: (0, 1), 5: (1, 2), 6: (2, 3), 8: (3, 4)}
+LATE_B = {1: (4, 5), 2: (5, 6), 3: (6, 7), 4: (7, 8)}
 QUERY_AT = 4
-UNITS_C = {4: (0, 1), 5: (1, 3), 6: (3, 5), 7: (5, 7)}
+UNITS_C = {4: (0, 1), 5: (1, 3), 6: (3, 5), 7: (5, 7), 8: (7, 8)}
 
 
 def rope_tables(pos):
@@ -47,20 +52,11 @@
     return v * cosine + pltpu.roll(v, HEAD_DIM // 2, 1) * sine
 
 
-def bounds(table, s):
-    if isinstance(s, int):
-        return table.get(s, (0, 0))
+def over(table, s, f):
     low, high = jnp.int32(0), jnp.int32(0)
     for k, (a, b) in table.items():
         low = jnp.where(s == k, a, low)
         high = jnp.where(s == k, b, high)
-    return low, high
-
-
-def over(table, s, f):
-    low, high = bounds(table, s)
-    if isinstance(s, int) and low == high:
-        return
 
     def one(u, _):
         f(u)
@@ -138,17 +134,19 @@
 
     def pieces(phase):
         if phase == 2:
-            found = [(6 + k % 2, 1, k // 2 * (depth // 2), depth // 2, False) for k in range(4)]
+            found = [(6 + k % 2, 1, k // 2 * (depth // 2), depth // 2) for k in range(4)]
         else:
-            extra = EXTRA[phase]
-            found = [
-                (stream, count, odd * (depth - extra), extra, True) if own else (stream, count, extra, depth - 2 * extra, False)
-                for stream, count, own in PARTS[phase]
-            ]
+            found = []
+            for stream, count, own in PARTS[phase]:
+                extra = EXTRA[0 if stream in GROUPS[0] else 1]
+                if own:
+                    found.append((stream, count, odd * (depth - extra), extra))
+                else:
+                    found.append((stream, count, extra, depth - 2 * extra))
         return [(LANES[phase] + 2 * k, *piece) for k, piece in enumerate(found)]
 
     def hop(piece, way, s):
-        lane, stream, streams, first, count, _ = piece
+        lane, stream, streams, first, count = piece
         owner = lax.rem(me + shards - (s - 1), shards) if way == 0 else lax.rem(me + (s - 1), shards)
         if isinstance(s, int) and s == far:
             upper = (count // 2 + 15) // 16 * 16
@@ -163,16 +161,21 @@
             device_id={"shard": right if way == 0 else left}, device_id_type=MESH,
         )
 
-    def hand(phase, v):
-        extra = EXTRA[phase]
-        streams = PHASES[phase]
+    def hand(k, v):
+        _, _, stream, streams = HANDS[k]
+        extra = EXTRA[0 if stream in GROUPS[0] else 1]
         ref = buf.at[
-            pl.ds(streams[0], len(streams)), owner_of(v), pl.ds(pl.multiple_of(odd * (depth - extra), 16), extra)
+            pl.ds(stream, streams), owner_of(v), pl.ds(pl.multiple_of(odd * (depth - extra), 16), extra)
         ]
         return pltpu.make_async_remote_copy(
-            src_ref=ref, dst_ref=ref, send_sem=ysend_sem.at[phase, v], recv_sem=yrecv_sem.at[phase, v],
+            src_ref=ref, dst_ref=ref, send_sem=ysend_sem.at[k, v], recv_sem=yrecv_sem.at[k, v],
             device_id={"groups": twin}, device_id_type=MESH,
         )
+
+    def hands(phase, part, v):
+        for k, (at, after, _, _) in enumerate(HANDS):
+            if at == phase and after == part:
+                hand(k, v).start()
 
     def draft_hop(way, s):
         owner = lax.rem(me + shards - (s - 1), shards) if way == 0 else lax.rem(me + (s - 1), shards)
@@ -190,9 +193,7 @@
                 draft_hop(way, 1).start()
 
     def pass_on(phase, s):
-        found = pieces(phase)
-        owns = sum(piece[-1] for piece in found)
-        for k, piece in enumerate(found):
+        for k, piece in enumerate(pieces(phase)):
             for way in range(2):
                 hop(piece, way, s).wait_recv()
                 hop(piece, way, s).wait_send()
@@ -205,8 +206,7 @@
                 def _():
                     hop(piece, way, far).start()
 
-                if k == owns - 1:
-                    hand(phase, 2 * s - 1 + way).start()
+                hands(phase, k, 2 * s - 1 + way)
         if phase == 0:
             for way in range(2):
                 draft_hop(way, s).wait_recv()
@@ -218,32 +218,39 @@
             def _():
                 draft_hop(1, s + 1).start()
 
+        if phase < 2:
+
+            @pl.when(s == far - 1)
+            def _():
+                launch(phase + 1)
+
     def finish(phase):
-        found = pieces(phase)
-        owns = sum(piece[-1] for piece in found)
-        for k, piece in enumerate(found):
+        for k, piece in enumerate(pieces(phase)):
             for way in range(2):
                 hop(piece, way, far).wait_recv()
                 hop(piece, way, far).wait_send()
-            if k == owns - 1:
-                hand(phase, 2 * far - 1).start()
+            hands(phase, k, 2 * far - 1)
         if phase == 0:
             draft_hop(0, far).wait_recv()
             draft_hop(0, far).wait_send()
 
-    def ring(phase, work, ready_next):
+    def ring(phase, work):
         def step(s, _):
-            pass_on(phase, s)
+            @pl.when(s < far)
+            def _():
+                pass_on(phase, s)
+
+            @pl.when(s == far)
+            def _():
+                finish(phase)
+
             work(s)
             return 0
 
-        lax.fori_loop(1, far, step, 0)
-        ready_next()
-        finish(phase)
-        work(far)
+        lax.fori_loop(1, far + 1, step, 0)
 
     def multiply(phase, u):
-        streams = PHASES[phase]
+        streams = GROUPS[phase]
 
         def one(v, _):
             owner = owner_of(v)
@@ -254,7 +261,8 @@
 
             @pl.when(v > 0)
             def _():
-                hand(phase, v).wait_recv()
+                for k in NEEDS[phase]:
+                    hand(k, v).wait_recv()
 
             w = jnp.concatenate([buf[stream, owner] for stream in streams], 1)
             got = jnp.dot(xs[owner], w, preferred_element_type=F32)
@@ -271,8 +279,8 @@
             pos = jnp.where(row >= j * BLK, row - j * BLK + map_ref[me * per + j] * BLK, pos)
         return pos
 
-    loads[0].wait()
-    loads[1].wait()
+    for load in loads[:3]:
+        load.wait()
     launch(0)
 
     for stream in range(6):
@@ -301,12 +309,9 @@
     limit[0 : G * rows] = jnp.broadcast_to(own_rows(G * rows), (G * rows, HEAD_DIM))
     limit[G * rows : high] = jnp.full((DRAFT_ROWS, HEAD_DIM), FAR - 1, jnp.int32)
 
-    def next0():
-        for load in loads[2:]:
-            load.wait()
-        launch(1)
-
-    ring(0, lambda s: over(UNITS_A, s, functools.partial(multiply, 0)), next0)
+    for load in loads[3:]:
+        load.wait()
+    ring(0, lambda s: over(UNITS_A, s, functools.partial(multiply, 0)))
 
     def own_cache():
         def one(b, _):
@@ -322,12 +327,11 @@
         dkv[1] = acc[1, tall : tall + drafts, :].astype(BF16)
 
     def work1(s):
-        if not isinstance(s, int):
-            over(LATE_A, s, functools.partial(multiply, 0))
-            pl.when(s == CACHE_AT)(own_cache)
+        over(LATE_A, s, functools.partial(multiply, 0))
+        pl.when(s == CACHE_AT)(own_cache)
         over(UNITS_B, s, functools.partial(multiply, 1))
 
-    ring(1, work1, lambda: launch(2))
+    ring(1, work1)
 
     def queries():
         dq = [rope(acc[2 + g, tall : tall + drafts, :], dcos[...], dsin[...]) for g in range(G)]
@@ -375,41 +379,7 @@
 
         lax.fori_loop(0, seqs, one, 0)
 
-    def work2(s):
-        if not isinstance(s, int):
-            over(LATE_B, s, functools.partial(multiply, 1))
-            pl.when(s == QUERY_AT)(queries)
-        over(UNITS_C, s, attend)
-
-    ring(2, work2, lambda: None)
-
-    attend(far - 1, ((G * rows, high),))
-    wo_load.wait()
-    r = lax.broadcasted_iota(jnp.int32, (DRAFT_ROWS, drafts), 0)
-    c = lax.broadcasted_iota(jnp.int32, (DRAFT_ROWS, drafts), 1)
-    for b in range(seqs):
-        at_r = slice(G * rows, high)
-        new = lax.dot_general(qbuf[b, at_r], dkv[0], (((1,), (1,)), ((), ())), preferred_element_type=F32)
-        seen = (lax.rem(c, seqs) == b) & (c // seqs <= lax.rem(r, steps))
-        new = jnp.where(seen, new, NEG)
-        before = mbuf[b, at_r][:, 0:1]
-        top = jnp.maximum(before, jnp.max(new, 1, keepdims=True))
-        shrink = jnp.exp2((before - top) * factor)
-        w = jnp.where(seen, jnp.exp2((new - top) * factor), 0.0)
-        total = jnp.sum(lbuf[b, at_r], 1, keepdims=True) * shrink + jnp.sum(w, 1, keepdims=True)
-        mixed = obuf[b, at_r] * shrink + jnp.dot(w.astype(BF16), dkv[1], preferred_element_type=F32)
-        attn = (mixed / total).astype(BF16).astype(F32)
-        aflat[b * G * steps : (b + 1) * G * steps] = attn[0 : G * steps]
-    for g in range(G):
-        for t in range(steps):
-            lhs[t * seqs : (t + 1) * seqs, g * HEAD_DIM : (g + 1) * HEAD_DIM] = aflat[
-                pl.ds(g * steps + t, seqs, stride=G * steps), :
-            ]
-    partial = jnp.dot(lhs[...].astype(BF16), wo[...], preferred_element_type=F32)
-    wide = partial.shape[1] // heads
-    for h in range(heads):
-        part[h] = partial[:, h * wide : (h + 1) * wide]
-    parts[place] = part[head]
+    wide = wo.shape[1] // heads
 
     def give(k):
         other = lax.rem(place + k, peers)
@@ -418,18 +388,52 @@
             device_id={"head": other // pairs, "pair": other % pairs}, device_id_type=MESH,
         )
 
-    r1 = lax.broadcasted_iota(jnp.int32, (seqs * G * steps, 1), 0)
-    mine = jnp.zeros((seqs * G * steps, 1), jnp.int32)
-    for p in range(seqs * G):
-        mine = jnp.where(r1 // steps == p, owner_ref[0, p], mine)
-    picked = jnp.where(mine == me, aflat[...], 0.0)
-    found = [jnp.sum(jnp.where(lax.rem(r1, steps) == t, picked, 0.0), 0, keepdims=True) for t in range(steps)]
-    dattn_ref[0, 0] = jnp.concatenate(found, 0).astype(BF16)
-
-    for k in range(1, peers):
-        give(k).start()
-
-    attend(far - 1, ((0, 2 * rows), (2 * rows, 4 * rows)))
+    def draft_outputs():
+        attend(far - 1, ((G * rows, high),))
+        wo_load.wait()
+        r = lax.broadcasted_iota(jnp.int32, (DRAFT_ROWS, drafts), 0)
+        c = lax.broadcasted_iota(jnp.int32, (DRAFT_ROWS, drafts), 1)
+        for b in range(seqs):
+            at_r = slice(G * rows, high)
+            new = lax.dot_general(qbuf[b, at_r], dkv[0], (((1,), (1,)), ((), ())), preferred_element_type=F32)
+            seen = (lax.rem(c, seqs) == b) & (c // seqs <= lax.rem(r, steps))
+            new = jnp.where(seen, new, NEG)
+            before = mbuf[b, at_r][:, 0:1]
+            top = jnp.maximum(before, jnp.max(new, 1, keepdims=True))
+            shrink = jnp.exp2((before - top) * factor)
+            w = jnp.where(seen, jnp.exp2((new - top) * factor), 0.0)
+            total = jnp.sum(lbuf[b, at_r], 1, keepdims=True) * shrink + jnp.sum(w, 1, keepdims=True)
+            mixed = obuf[b, at_r] * shrink + jnp.dot(w.astype(BF16), dkv[1], preferred_element_type=F32)
+            attn = (mixed / total).astype(BF16).astype(F32)
+            aflat[b * G * steps : (b + 1) * G * steps] = attn[0 : G * steps]
+        for g in range(G):
+            for t in range(steps):
+                lhs[t * seqs : (t + 1) * seqs, g * HEAD_DIM : (g + 1) * HEAD_DIM] = aflat[
+                    pl.ds(g * steps + t, seqs, stride=G * steps), :
+                ]
+        partial = jnp.dot(lhs[...].astype(BF16), wo[...], preferred_element_type=F32)
+        for h in range(heads):
+            part[h] = partial[:, h * wide : (h + 1) * wide]
+        parts[place] = part[head]
+
+        r1 = lax.broadcasted_iota(jnp.int32, (seqs * G * steps, 1), 0)
+        mine = jnp.zeros((seqs * G * steps, 1), jnp.int32)
+        for p in range(seqs * G):
+            mine = jnp.where(r1 // steps == p, owner_ref[0, p], mine)
+        picked = jnp.where(mine == me, aflat[...], 0.0)
+        found = [jnp.sum(jnp.where(lax.rem(r1, steps) == t, picked, 0.0), 0, keepdims=True) for t in range(steps)]
+        dattn_ref[0, 0] = jnp.concatenate(found, 0).astype(BF16)
+
+        for k in range(1, peers):
+            give(k).start()
+
+    def work2(s):
+        over(LATE_B, s, functools.partial(multiply, 1))
+        pl.when(s == QUERY_AT)(queries)
+        pl.when(s == far)(draft_outputs)
+        over(UNITS_C, s, attend)
+
+    ring(2, work2)
 
     def put(b, _):
         for g in range(G):
@@ -458,8 +462,8 @@
         give(k).wait_send()
 
     def drain(v, _):
-        for phase in range(2):
-            hand(phase, v).wait_send()
+        for k in range(len(HANDS)):
+            hand(k, v).wait_send()
         return 0
 
     lax.fori_loop(1, shards, drain, 0)
@@ -519,10 +523,10 @@
             dma((7,)),
             dma((shards,)),
             dma((1,)),
-            dma((14,)),
-            dma((14, TURNS)),
-            dma((2, shards)),
-            dma((2, shards)),
+            dma((20,)),
+            dma((20, TURNS)),
+            dma((len(HANDS), shards)),
+            dma((len(HANDS), shards)),
             dma((2,)),
             dma((2, shards // 2)),
             dma((peers,)),

time: 169 us -> 167 us (0.988)
  Pallas kernels: 168 us -> 166 us
    pallas_call x1, Pallas kernels: 166 us -> 164 us  [body(): pl.pallas_call(functools.partial(kernel, groups, shards, heads, pairs), o...]
where the time goes in v5:
time: 167 us
  Pallas kernels  166 us (99%)
    pallas_call x1, Pallas kernels, body(): pl.pallas_call(functools.partial(kernel, groups, shards, heads, pairs), o...  164 us

profile of v5, /device:TPU:33, one launch (start us, length us, event | category | flops | bytes accessed | tf_op | source)
XLA Modules:
  0.0 167.0 jit_solution(7208711234213479653)
XLA Ops:
  0.6 164.4 %shard_map.112 = (bf16[128,4,512]{2,1,0:T(4,128)(2,1)}, bf16[1,1,2,128]{3,2,1,0:T(2,128)(2,1)}, bf16[2,4,64]{2,1,0:T(4,128)(2,1)}) custom-call(bf16[128,4,8192]{2,1,0:T(4,128)(2,1)} %x_hbm.1, bf16[2,4,512]{2,1,0:T(4,128)(2,1)} %d_ref.1, bf16[512,512]{1,0:T(8,128)(2,1)} %wq_hbm.1, bf16[512,128]{1,0:T(8,128)(2,1)} %wk_hbm.1, bf16[512,128]{1,0:T(8,128)(2,1)} %wv_hbm.1, ...), custom_call_target="tpu_custom_call" | custom-call | tf_op jit(solution)/shard_map/pallas_call | solution.py:490
  165.1 1.9 %shard_map.113 = (bf16[128,4,512]{2,1,0:T(4,128)(2,1)}, bf16[1,1,2,128]{3,2,1,0:T(2,128)(2,1)}, bf16[2,4,64]{2,1,0:T(4,128)(2,1)}) custom-call(bf16[128,4,512]{2,1,0:T(4,128)(2,1)} %get-tuple-element.9.refs_0_, bf16[1,1,2,128]{3,2,1,0:T(2,128)(2,1)} %get-tuple-element.10.refs_1_, bf16[2,4,64]{2,1,0:T(4,128)(2,1)} %get-tuple-element.11.refs_2_), custom_call_target="tpu_custom_call" | custom-call | tf_op jit(solution)/shard_map/pallas_call | solution.py:539

commit v6 on v5

--- a/solution.py
+++ b/solution.py
@@ -19,14 +19,14 @@
 FAR = 1 << 30
 DRAFT_ROWS = 16
 
-GROUPS = ((0, 1), (2, 3, 4, 5))
+GROUPS = ((0, 1), (2,), (3, 4, 5))
 EXTRA = (176, 208)
 PARTS = (
     ((0, 1, True), (1, 1, True), (2, 1, True), (0, 1, False), (1, 1, False)),
     ((3, 1, True), (4, 1, True), (5, 1, True), (2, 2, False), (4, 2, False)),
 )
 HANDS = ((0, 1, 0, 2), (0, 2, 2, 1), (1, 2, 3, 3))
-NEEDS = ((0,), (1, 2))
+NEEDS = ((0,), (1,), (2,))
 LANES = (0, 10, 0)
 TURNS = 4
 UNITS_A = {2: (0, 1), 3: (1, 2), 4: (2, 3), 6: (3, 4), 7: (4, 5), 8: (5, 6)}
@@ -35,7 +35,8 @@
 UNITS_B = {4: (0, 1), 5: (1, 2), 6: (2, 3), 8: (3, 4)}
 LATE_B = {1: (4, 5), 2: (5, 6), 3: (6, 7), 4: (7, 8)}
 QUERY_AT = 4
-UNITS_C = {4: (0, 1), 5: (1, 3), 6: (3, 5), 7: (5, 7), 8: (7, 8)}
+UNITS_C = {4: (0, 2), 5: (2, 4), 6: (4, 6), 7: (6, 7), 8: (7, 8)}
+UNITS_HEAD = {s: (s - 1, s) for s in range(1, 9)}
 
 
 def rope_tables(pos):
@@ -249,19 +250,19 @@
 
         lax.fori_loop(1, far + 1, step, 0)
 
-    def multiply(phase, u):
-        streams = GROUPS[phase]
+    def multiply(group_at, u):
+        streams = GROUPS[group_at]
 
         def one(v, _):
             owner = owner_of(v)
-            if phase == 0:
+            if group_at == 0:
                 x_load(owner).wait()
                 xs[owner, 0:tall] = xin[owner].reshape(tall, depth)
                 xs[owner, tall : tall + drafts] = dbuf[owner]
 
             @pl.when(v > 0)
             def _():
-                for k in NEEDS[phase]:
+                for k in NEEDS[group_at]:
                     hand(k, v).wait_recv()
 
             w = jnp.concatenate([buf[stream, owner] for stream in streams], 1)
@@ -329,9 +330,24 @@
     def work1(s):
         over(LATE_A, s, functools.partial(multiply, 0))
         pl.when(s == CACHE_AT)(own_cache)
-        over(UNITS_B, s, functools.partial(multiply, 1))
+        over(UNITS_HEAD, s, functools.partial(multiply, 1))
+        over(UNITS_B, s, functools.partial(multiply, 2))
 
     ring(1, work1)
+
+    def rotated(b, g):
+        q = acc[2 + g, pl.ds(b, rows, stride=seqs), :]
+        qbuf[b, g * rows : (g + 1) * rows] = rope(q, cosb[...], sinb[...]).astype(BF16)
+
+    def first_queries():
+        def one(b, _):
+            rotated(b, 0)
+            mbuf[b] = jnp.full((high, HEAD_DIM), NEG, F32)
+            lbuf[b] = jnp.zeros((high, HEAD_DIM), F32)
+            obuf[b] = jnp.zeros((high, HEAD_DIM), F32)
+            return 0
+
+        lax.fori_loop(0, seqs, one, 0)
 
     def queries():
         dq = [rope(acc[2 + g, tall : tall + drafts, :], dcos[...], dsin[...]) for g in range(G)]
@@ -341,17 +357,16 @@
             qbuf[b, G * rows : high] = jnp.concatenate(pieces, 0).astype(BF16)
 
         def one(b, _):
-            for g in range(G):
-                q = acc[2 + g, pl.ds(b, rows, stride=seqs), :]
-                qbuf[b, g * rows : (g + 1) * rows] = rope(q, cosb[...], sinb[...]).astype(BF16)
-            mbuf[b] = jnp.full((high, HEAD_DIM), NEG, F32)
-            lbuf[b] = jnp.zeros((high, HEAD_DIM), F32)
-            obuf[b] = jnp.zeros((high, HEAD_DIM), F32)
+            for g in range(1, G):
+                rotated(b, g)
             return 0
 
         lax.fori_loop(0, seqs, one, 0)
 
-    def attend(u, tiles=((0, high // 3), (high // 3, high // 3 * 2), (high // 3 * 2, high))):
+    middle = rows + (high - rows) // 32 * 16
+    rest = ((rows, middle), (middle, high))
+
+    def attend(u, tiles=rest):
         first, second = owner_of(2 * u), owner_of(2 * u + 1)
 
         def one(b, _):
@@ -428,9 +443,11 @@
             give(k).start()
 
     def work2(s):
-        over(LATE_B, s, functools.partial(multiply, 1))
+        pl.when(s == 1)(first_queries)
+        over(LATE_B, s, functools.partial(multiply, 2))
         pl.when(s == QUERY_AT)(queries)
         pl.when(s == far)(draft_outputs)
+        over(UNITS_HEAD, s, functools.partial(attend, tiles=((0, rows),)))
         over(UNITS_C, s, attend)
 
     ring(2, work2)

time: 167 us -> 173 us (1.036)
  Pallas kernels: 166 us -> 171 us
    pallas_call x1, Pallas kernels: 164 us -> 169 us  [body(): pl.pallas_call(functools.partial(kernel, groups, shards, heads, pairs), o...]
where the time goes in v6:
time: 173 us; the launch traced here: 172 us
  Pallas kernels  171 us (99%)
    pallas_call x1, Pallas kernels, body(): pl.pallas_call(functools.partial(kernel, groups, shards, heads, pairs), o...  169 us

profile of v6, /device:TPU:33, one launch (start us, length us, event | category | flops | bytes accessed | tf_op | source)
XLA Modules:
  0.0 171.8 jit_solution(14162745108853961069)
XLA Ops:
  0.6 169.3 %shard_map.112 = (bf16[128,4,512]{2,1,0:T(4,128)(2,1)}, bf16[1,1,2,128]{3,2,1,0:T(2,128)(2,1)}, bf16[2,4,64]{2,1,0:T(4,128)(2,1)}) custom-call(bf16[128,4,8192]{2,1,0:T(4,128)(2,1)} %x_hbm.1, bf16[2,4,512]{2,1,0:T(4,128)(2,1)} %d_ref.1, bf16[512,512]{1,0:T(8,128)(2,1)} %wq_hbm.1, bf16[512,128]{1,0:T(8,128)(2,1)} %wk_hbm.1, bf16[512,128]{1,0:T(8,128)(2,1)} %wv_hbm.1, ...), custom_call_target="tpu_custom_call" | custom-call | tf_op jit(solution)/shard_map/pallas_call | solution.py:507
  169.9 1.9 %shard_map.113 = (bf16[128,4,512]{2,1,0:T(4,128)(2,1)}, bf16[1,1,2,128]{3,2,1,0:T(2,128)(2,1)}, bf16[2,4,64]{2,1,0:T(4,128)(2,1)}) custom-call(bf16[128,4,512]{2,1,0:T(4,128)(2,1)} %get-tuple-element.9.refs_0_, bf16[1,1,2,128]{3,2,1,0:T(2,128)(2,1)} %get-tuple-element.10.refs_1_, bf16[2,4,64]{2,1,0:T(4,128)(2,1)} %get-tuple-element.11.refs_2_), custom_call_target="tpu_custom_call" | custom-call | tf_op jit(solution)/shard_map/pallas_call | solution.py:556

commit v7 on v5

--- a/solution.py
+++ b/solution.py
@@ -351,7 +351,7 @@
 
         lax.fori_loop(0, seqs, one, 0)
 
-    def attend(u, tiles=((0, high // 3), (high // 3, high // 3 * 2), (high // 3 * 2, high))):
+    def attend(u, tiles=((0, high),)):
         first, second = owner_of(2 * u), owner_of(2 * u + 1)
 
         def one(b, _):

time: 167 us -> 165 us (0.988)
  Pallas kernels: 166 us -> 164 us
    pallas_call x1, Pallas kernels: 164 us -> 162 us  [body(): pl.pallas_call(functools.partial(kernel, groups, shards, heads, pairs), o...]
where the time goes in v7:
time: 165 us
  Pallas kernels  164 us (99%)
    pallas_call x1, Pallas kernels, body(): pl.pallas_call(functools.partial(kernel, groups, shards, heads, pairs), o...  162 us

profile of v7, /device:TPU:33, one launch (start us, length us, event | category | flops | bytes accessed | tf_op | source)
XLA Modules:
  0.0 164.6 jit_solution(17697032804525019511)
XLA Ops:
  0.6 162.1 %shard_map.112 = (bf16[128,4,512]{2,1,0:T(4,128)(2,1)}, bf16[1,1,2,128]{3,2,1,0:T(2,128)(2,1)}, bf16[2,4,64]{2,1,0:T(4,128)(2,1)}) custom-call(bf16[128,4,8192]{2,1,0:T(4,128)(2,1)} %x_hbm.1, bf16[2,4,512]{2,1,0:T(4,128)(2,1)} %d_ref.1, bf16[512,512]{1,0:T(8,128)(2,1)} %wq_hbm.1, bf16[512,128]{1,0:T(8,128)(2,1)} %wk_hbm.1, bf16[512,128]{1,0:T(8,128)(2,1)} %wv_hbm.1, ...), custom_call_target="tpu_custom_call" | custom-call | tf_op jit(solution)/shard_map/pallas_call | solution.py:490
  162.7 1.9 %shard_map.113 = (bf16[128,4,512]{2,1,0:T(4,128)(2,1)}, bf16[1,1,2,128]{3,2,1,0:T(2,128)(2,1)}, bf16[2,4,64]{2,1,0:T(4,128)(2,1)}) custom-call(bf16[128,4,512]{2,1,0:T(4,128)(2,1)} %get-tuple-element.9.refs_0_, bf16[1,1,2,128]{3,2,1,0:T(2,128)(2,1)} %get-tuple-element.10.refs_1_, bf16[2,4,64]{2,1,0:T(4,128)(2,1)} %get-tuple-element.11.refs_2_), custom_call_target="tpu_custom_call" | custom-call | tf_op jit(solution)/shard_map/pallas_call | solution.py:539
